TPU v7x, 256 devices: a whole 4x4x8 slice. The times are simulated.
256 devices in a mesh: dp: 32 (over x, y, z_lo), seq: 8 (over z_hi, core).
Axes of the slice: x: 4, y: 4, z: 8 (z_hi: 4, z_lo: 2; z = z_hi * 2 + z_lo), core: 2. Of those that a mesh axis runs over, the one named last changes fastest.
Arguments:
- frames: bfloat16 [32, 4096, 512], P('dp', 'seq'), may hold values from -6 to 6
- cotangent: bfloat16 [32, 4096, 512], P('dp', 'seq'), may hold values from -6 to 6
- weight_in: bfloat16 [2, 512, 2176], replicated, may hold values from -0.25 to 0.25
- qk_scales: float32 [2, 2, 128], replicated, may hold values from 0.5 to 1.5
- weight_out: bfloat16 [2, 1024, 512], replicated, may hold values from -0.1875 to 0.1875
- gains: float32 [2, 512], replicated, may hold values from 0.5 to 1.5
Outputs:
- output: bfloat16 [32, 4096, 512], P('dp', 'seq')
- grad_frames: bfloat16 [32, 4096, 512], P('dp', 'seq')
- grad_in: float32 [2, 512, 2176], P(None, 'dp')
- grad_out: float32 [2, 1024, 512], P(None, 'dp')
- grad_gains: float32 [2, 512], replicated
- grad_scales: float32 [2, 2, 128], replicated
All inputs are finite; a program needn't handle non-finite values.
Results may differ from a plain program's by a relative error of at most 0.028.
Values may be sent and summed in bfloat16 or wider, within the bound.
A program may use at most 192 MiB of HBM per device.

v0:
```python
from functools import partial
import functools

import jax
import jax.numpy as jnp
from jax import lax
from jax.sharding import Mesh
from jax.sharding import PartitionSpec as P

BLOCK = 256
DP = ("dp_0", "dp_1", "dp_2")
SEQ = ("seq_0", "seq_1")
DP_SEQ = ("dp_0", "dp_1", "dp_2", "seq_0", "seq_1")


EPSILON = 1e-06


def in_order(parts, dim):
    parts = jnp.moveaxis(parts, 0, dim)
    shape = parts.shape
    return parts.reshape(*shape[:dim], shape[dim] * shape[dim + 1], *shape[dim + 2 :])


def one_gather(arrays, axis, dims):
    ravelled = jnp.concatenate([a.reshape(-1) for a in arrays])
    lines, at, gathered = (lax.all_gather(ravelled, axis), 0, [])
    for a, dim in zip(arrays, dims):
        parts = lines[:, at : at + a.size].reshape(-1, *a.shape)
        gathered.append(in_order(parts, dim))
        at += a.size
    return tuple(gathered)


def over_axes(x, axes):
    return functools.reduce(lax.psum, axes, x)


def normed(values, gain_row):
    scaling = lax.rsqrt(jnp.mean(values * values, axis=-1, keepdims=True) + EPSILON)
    return values * scaling * gain_row


def mixer(projected, scale_pair, attend_axis):
    width = (projected.shape[-1] - scale_pair.shape[-1]) // 2
    active = jax.nn.silu(projected)
    gate_part = active[..., :width]
    value_part = active[..., width : 2 * width].astype(jnp.bfloat16)
    shared = active[..., 2 * width :]
    query = (shared * scale_pair[0]).astype(jnp.bfloat16)
    keyed = (shared * scale_pair[1]).astype(jnp.bfloat16)
    length = projected.shape[attend_axis]
    if attend_axis == 1:
        score_form = "gls,gms->glm"
        mix_form = "glm,gme->gle"
    else:
        score_form = "lgs,mgs->glm"
        mix_form = "glm,mge->lge"
    scores = jnp.einsum(score_form, query, keyed, preferred_element_type=jnp.float32)
    scores = scores * scale_pair.shape[-1] ** (-0.5)
    weights = (jnp.square(jax.nn.relu(scores)) / length).astype(jnp.bfloat16)
    mixed = jnp.einsum(mix_form, weights, value_part, preferred_element_type=jnp.float32)
    return (gate_part * mixed).astype(jnp.bfloat16)


def rows_product(left, right):
    left_rows = left.reshape(-1, left.shape[-1])
    right_rows = right.reshape(-1, right.shape[-1])
    return lax.dot_general(
        left_rows, right_rows, (((0,), (0,)), ((), ())), preferred_element_type=jnp.float32
    )


def against(values, weight):
    return lax.dot_general(
        values, weight, (((values.ndim - 1,), (1,)), ((), ())), preferred_element_type=jnp.float32
    )


def unit_forward(inputs_now, weight_in, scale_pair, weight_out, gain_row, attend_axis):
    hidden = normed(inputs_now.astype(jnp.float32), gain_row).astype(jnp.bfloat16)
    projected = jnp.dot(hidden, weight_in, preferred_element_type=jnp.float32)
    gated = mixer(projected, scale_pair, attend_axis)
    result = (
        inputs_now.astype(jnp.float32)
        + jnp.dot(gated, weight_out, preferred_element_type=jnp.float32)
    ).astype(jnp.bfloat16)
    return (result, (hidden, projected, gated))


def unit_backward(
    inputs_now, upstream, weight_in, scale_pair, weight_out, gain_row, saved, attend_axis
):
    hidden, projected, gated = saved
    grad_out = rows_product(gated, upstream)
    grad_gated = against(upstream, weight_out).astype(jnp.bfloat16)
    pulled = jax.vjp(partial(mixer, attend_axis=attend_axis), projected, scale_pair)[1]
    grad_proj, grad_scale = pulled(grad_gated)
    grad_proj = grad_proj.astype(jnp.bfloat16)
    grad_in = rows_product(hidden, grad_proj)
    grad_hidden = against(grad_proj, weight_in)
    norm_pull = jax.vjp(normed, inputs_now.astype(jnp.float32), gain_row)[1]
    grad_inputs, grad_gain = norm_pull(grad_hidden)
    grad_inputs = (upstream.astype(jnp.float32) + grad_inputs).astype(jnp.bfloat16)
    return (grad_inputs, grad_in, grad_out, grad_gain, grad_scale)


def on_device(frames, cotangent, weight_in, qk_scales, weight_out, gains):
    block_count = frames.shape[1] // BLOCK
    width = frames.shape[2]
    tokens_all = frames.shape[0] * frames.shape[1] * lax.axis_size(DP) * lax.axis_size(SEQ)
    scaling = tokens_all ** (-0.5)
    blocked = frames.reshape(block_count, BLOCK, width)
    first, saved_first = unit_forward(
        blocked, weight_in[0], qk_scales[0], weight_out[0], gains[0], 1
    )
    first_pos = lax.all_to_all(first, SEQ, split_axis=1, concat_axis=0, tiled=True)
    second, saved_second = unit_forward(
        first_pos, weight_in[1], qk_scales[1], weight_out[1], gains[1], 0
    )
    result = lax.all_to_all(second, SEQ, split_axis=0, concat_axis=1, tiled=True)
    upstream = lax.all_to_all(
        cotangent.reshape(block_count, BLOCK, width), SEQ, split_axis=1, concat_axis=0, tiled=True
    )
    back_pos, in_late, out_late, gain_late, scale_late = unit_backward(
        first_pos, upstream, weight_in[1], qk_scales[1], weight_out[1], gains[1], saved_second, 0
    )
    back_first = lax.all_to_all(back_pos, SEQ, split_axis=0, concat_axis=1, tiled=True)
    back_frames, in_early, out_early, gain_early, scale_early = unit_backward(
        blocked, back_first, weight_in[0], qk_scales[0], weight_out[0], gains[0], saved_first, 1
    )
    grad_in = jnp.stack([in_early, in_late]) * scaling
    grad_out = jnp.stack([out_early, out_late]) * scaling
    grad_gains = jnp.stack([gain_early, gain_late]) * scaling
    grad_scales = jnp.stack([scale_early, scale_late]) * scaling
    shares = (
        lax.psum_scatter(grad_in, DP_SEQ, scatter_dimension=1, tiled=True),
        lax.psum_scatter(grad_out, DP_SEQ, scatter_dimension=1, tiled=True),
    )
    summed = tuple(
        (
            part.astype(jnp.float32)
            for part in one_gather(
                (shares[0].astype(jnp.bfloat16), shares[1].astype(jnp.bfloat16)), SEQ, (1, 1)
            )
        )
    )
    small = (over_axes(grad_gains, DP_SEQ), over_axes(grad_scales, DP_SEQ))
    return (
        result.reshape(frames.shape),
        back_frames.reshape(frames.shape),
        summed[0],
        summed[1],
        small[0],
        small[1],
    )


def solution(mesh):
    split = Mesh(mesh.devices.reshape(4, 4, 2, 4, 2), ("dp_0", "dp_1", "dp_2", "seq_0", "seq_1"))
    placed = (P(DP, SEQ, None), P(DP, SEQ, None), P(), P(), P(), P())
    return jax.shard_map(
        on_device,
        mesh=split,
        in_specs=placed,
        out_specs=(
            P(DP, SEQ, None),
            P(DP, SEQ, None),
            P(None, DP, None),
            P(None, DP, None),
            P(),
            P(),
        ),
        check_vma=False,
    )
```

profile of v0, /device:TPU:1, one launch (start us, length us, event | category | flops | bytes accessed | tf_op | source)
XLA Modules:
  0.0 347.1 jit_solution(11623062730977402469)
XLA Ops:
  0.6 2.4 copy.120
  3.0 10.0 %all-to-all-start.2 = ((bf16[2,256,512]{2,0,1:T(2,128)(2,1)}), bf16[2,256,512]{2,0,1:T(2,128)(2,1)S(1)}, u32[]{:S(2)}, u32[]{:S(2)}) async-start(bf16[2,256,512]{2,0,1:T(2,128)(2,1)} %copy.120), calls=%async_computation.2 | async-start | bytes 1048576 | tf_op jit(solution)/shard_map/all_to_all | solution.py:122
  17.0 5.4 %fusion.7 = (f32[2,256,2176]{2,1,0:T(8,128)S(1)}, f32[2,256,2176]{2,1,0:T(8,128)}) fusion(bf16[2,256,512]{2,1,0:T(8,128)(2,1)S(1)} %bitcast.191, bf16[2,512,2176]{2,1,0:T(8,128)(2,1)} %param.8), kind=kOutput, calls=%fused_computation.14 | convolution fusion | flops 1145307136 | bytes 11665408 | tf_op jit(solution)/shard_map/dot_general | solution.py:82
  22.6 1.8 multiply_convert_fusion
  24.4 1.6 copy-done.12
  28.0 7.2 %all-to-all-start = ((bf16[2,256,512]{2,0,1:T(2,128)(2,1)}), bf16[2,256,512]{2,0,1:T(2,128)(2,1)S(1)}, u32[]{:S(2)}, u32[]{:S(2)}) async-start(bf16[2,256,512]{2,0,1:T(2,128)(2,1)} %copy.113), calls=%async_computation | async-start | bytes 1048576 | tf_op jit(solution)/shard_map/all_to_all | solution.py:117
  36.9 2.0 convolution_convert_fusion.2
  38.9 10.5 %all-to-all-done = bf16[2,256,512]{2,0,1:T(2,128)(2,1)S(1)} async-done(((bf16[2,256,512]{2,0,1:T(2,128)(2,1)}), bf16[2,256,512]{2,0,1:T(2,128)(2,1)S(1)}, u32[]{:S(2)}, u32[]{:S(2)}) %all-to-all-start) | async-done | bytes 524320 | tf_op jit(solution)/shard_map/all_to_all | solution.py:117
  50.2 3.3 fusion.6
  62.3 1.8 fusion.2
  64.2 2.1 multiply_reduce_fusion
  67.4 8.0 %all-to-all-start.3 = ((bf16[16,32,512]{2,1,0:T(8,128)(2,1)}), bf16[16,32,512]{2,1,0:T(8,128)(2,1)}, u32[]{:S(2)}, u32[]{:S(2)}) async-start(bf16[16,32,512]{2,1,0:T(8,128)(2,1)} %fusion.56), calls=%async_computation.3 | async-start | bytes 1048576 | tf_op jit(solution)/shard_map/all_to_all | solution.py:128
  75.4 3.4 convolution_bitcast_fusion.2
  78.8 3.6 %convolution_bitcast_fusion = f32[1,512,2176]{2,1,0:T(8,128)} fusion(bf16[16,32,2176]{2,1,0:T(8,128)(2,1)S(1)} %fusion.2, f32[16,32,512]{2,1,0:T(8,128)S(1)} %bitcast.168, f32[16,32]{1,0:T(8,128)S(1)} %rsqrt.30, f32[512]{0:T(512)S(1)} %bitcast.202), kind=kOutput, calls=%fused_computation.3 | convolution fusion | flops 1141637120 | bytes 7737344 | tf_op jit(solution)/shard_map/dot_general | solution.py:69
  82.4 7.2 %all-to-all-done.3 = bf16[16,32,512]{2,1,0:T(8,128)(2,1)} async-done(((bf16[16,32,512]{2,1,0:T(8,128)(2,1)}), bf16[16,32,512]{2,1,0:T(8,128)(2,1)}, u32[]{:S(2)}, u32[]{:S(2)}) %all-to-all-start.3) | async-done | bytes 524320 | tf_op jit(solution)/shard_map/all_to_all | solution.py:128
  89.6 7.8 %all-to-all-start.1 = ((bf16[16,32,512]{2,1,0:T(8,128)(2,1)}), bf16[16,32,512]{2,1,0:T(8,128)(2,1)}, u32[]{:S(2)}, u32[]{:S(2)}) async-start(bf16[16,32,512]{2,1,0:T(8,128)(2,1)} %fusion.28), calls=%async_computation.1 | async-start | bytes 1048576 | tf_op jit(solution)/shard_map/all_to_all | solution.py:121
  98.6 2.8 convert_multiply_fusion
  101.4 2.1 convolution_convert_fusion
  106.0 2.7 maximum_multiply_fusion.1
  108.7 1.9 fusion.5
  110.6 1.5 convolution_bitcast_fusion.1
  112.2 4.2 %maximum_multiply_fusion = f32[2,512,2176]{2,1,0:T(8,128)} fusion(f32[1,512,2176]{2,1,0:T(8,128)S(1)} %bitcast.165, f32[1,512,2176]{2,1,0:T(8,128)S(1)} %convolution_bitcast_fusion.1), kind=kLoop, calls=%fused_computation | loop fusion | flops 4456448 | bytes 17825792 | tf_op jit(solution)/shard_map/mul | solution.py:132
  116.4 164.0 %all-reduce.19 = (bf16[2,1024,512]{2,1,0:T(8,128)(2,1)}, bf16[2,512,2176]{2,1,0:T(8,128)(2,1)}) all-reduce(f32[2,1024,512]{2,1,0:T(8,128)} %maximum_multiply_fusion.1, f32[2,512,2176]{2,1,0:T(8,128)} %maximum_multiply_fusion), channel_id=4, replica_groups=mesh['dp_0'=4,'dp_1'=4,'dp_2'=2,'seq_0'=4,'seq_1'=2] {'dp_0','dp_1','dp_..., use_global_device_ids=true, to_apply=%region_5.6.clone | all-reduce | flops 3276800 | bytes 19660800
  282.1 17.1 %all-gather.1 = bf16[8,1,12800]{2,1,0:T(2,128)(2,1)S(1)} all-gather(bf16[1,1,12800]{2,1,0:T(2,128)(2,1)S(1)} %reshape.173), channel_id=2, replica_groups=mesh['dp_0'=4,'dp_1'=4,'dp_2'=2,'seq_0'=4,'seq_1'=2] {'seq_0','seq_1'}, dimensions={0}, use_global_device_ids=true | all-gather | bytes 230400 | tf_op jit(solution)/shard_map/all_gather | solution.py:27
  299.3 4.7 %multiply_reduce_fusion.1 = (f32[512]{0:T(512)}, f32[2,256]{1,0:T(2,128)}, f32[2,256,512]{2,1,0:T(8,128)}) fusion(f32[2,256]{1,0:T(2,128)} %copy-done.15, f32[512]{0:T(512)} %bitcast.197, bf16[2,256,2176]{2,1,0:T(8,128)(2,1)S(1)} %fusion.5, bf16[2,512,2176]{2,1,0:T(8,128)(2,1)} %param.8, bf16[2,256,512]{2,1,0:T(8,128)(2,1)S(1)} %bitcast.171), kind=kOutput, calls=%fused_computation.88 | convolution fusion | flops 1142684672 | bytes 6037504 | tf_op jit(solution)/shard_map/dot_general | solution.py:75
  304.0 2.0 copy.119
  310.0 1.8 fusion.58
  311.9 7.0 %all-reduce.15 = (f32[2,512]{1,0:T(2,128)S(1)}, f32[2,2,128]{2,1,0:T(2,128)S(1)}) all-reduce(f32[2,512]{1,0:T(2,128)S(1)} %maximum_multiply_fusion.2, f32[2,2,128]{2,1,0:T(2,128)S(1)} %maximum_multiply_fusion.3), channel_id=1, replica_groups=mesh['dp_0'=4,'dp_1'=4,'dp_2'=2,'seq_0'=4,'seq_1'=2] {'dp_0'}, use_global_device_ids=true, to_apply=%region_8.9 | all-reduce | flops 1536 | bytes 12288 | tf_op jit(solution)/shard_map/psum | solution.py:36
  318.8 6.4 %all-reduce.14 = (f32[2,512]{1,0:T(2,128)S(1)}, f32[2,2,128]{2,1,0:T(2,128)S(1)}) all-reduce(f32[2,512]{1,0:T(2,128)S(1)} %get-tuple-element.38, f32[2,2,128]{2,1,0:T(2,128)S(1)} %get-tuple-element.39), channel_id=1, replica_groups=mesh['dp_0'=4,'dp_1'=4,'dp_2'=2,'seq_0'=4,'seq_1'=2] {'dp_1'}, use_global_device_ids=true, to_apply=%region_9.10 | all-reduce | flops 1536 | bytes 12288 | tf_op jit(solution)/shard_map/psum | solution.py:36
  325.3 3.8 %all-reduce.17 = (f32[2,512]{1,0:T(2,128)S(1)}, f32[2,2,128]{2,1,0:T(2,128)S(1)}) all-reduce(f32[2,512]{1,0:T(2,128)S(1)} %get-tuple-element.36, f32[2,2,128]{2,1,0:T(2,128)S(1)} %get-tuple-element.37), channel_id=1, replica_groups=mesh['dp_0'=4,'dp_1'=4,'dp_2'=2,'seq_0'=4,'seq_1'=2] {'dp_2'}, use_global_device_ids=true, to_apply=%region_10.11 | all-reduce | flops 1536 | bytes 12288 | tf_op jit(solution)/shard_map/psum | solution.py:36
  329.1 8.1 %all-reduce.13 = (f32[2,512]{1,0:T(2,128)S(1)}, f32[2,2,128]{2,1,0:T(2,128)S(1)}) all-reduce(f32[2,512]{1,0:T(2,128)S(1)} %get-tuple-element.42, f32[2,2,128]{2,1,0:T(2,128)S(1)} %get-tuple-element.43), channel_id=1, replica_groups=mesh['dp_0'=4,'dp_1'=4,'dp_2'=2,'seq_0'=4,'seq_1'=2] {'seq_0'}, use_global_device_ids=true, to_apply=%region_11.12 | all-reduce | flops 1536 | bytes 12288 | tf_op jit(solution)/shard_map/psum | solution.py:36
  337.2 10.0 %all-reduce.16 = (f32[2,512]{1,0:T(2,128)}, f32[2,2,128]{2,1,0:T(2,128)}) all-reduce(f32[2,512]{1,0:T(2,128)S(1)} %get-tuple-element.34, f32[2,2,128]{2,1,0:T(2,128)S(1)} %get-tuple-element.35), channel_id=1, replica_groups=mesh['dp_0'=4,'dp_1'=4,'dp_2'=2,'seq_0'=4,'seq_1'=2] {'seq_1'}, use_global_device_ids=true, to_apply=%region_12.13 | all-reduce | flops 1536 | bytes 12288 | tf_op jit(solution)/shard_map/psum | solution.py:36
  (113 shorter events, 27.8 us)
Async XLA Ops:
  3.0 25.0 %all-to-all-start.2 = ((bf16[2,256,512]{2,0,1:T(2,128)(2,1)}), bf16[2,256,512]{2,0,1:T(2,128)(2,1)S(1)}, u32[]{:S(2)}, u32[]{:S(2)}) async-start(bf16[2,256,512]{2,0,1:T(2,128)(2,1)} %copy.120), calls=%async_computation.2 | async-start | bytes 1048576 | tf_op jit(solution)/shard_map/all_to_all | solution.py:122
  15.7 94.9 %copy-start.14 = (f32[1,512]{1,0:T(1,128)}, f32[1,512]{1,0:T(1,128)S(1)}, u32[]{:S(2)}) copy-start(f32[1,512]{1,0:T(1,128)S(1)} %get-tuple-element.55) | copy-start | bytes 6148
  22.3 4.4 %copy-start = (f32[2,256,2176]{2,1,0:T(8,128)}, f32[2,256,2176]{2,1,0:T(8,128)S(1)}, u32[]{:S(2)}) copy-start(f32[2,256,2176]{2,1,0:T(8,128)S(1)} %get-tuple-element.62) | copy-start | bytes 13369348
  22.3 2.0 copy-start.2
  22.3 3.6 %copy-start.12 = (bf16[2,1024,512]{2,1,0:T(8,128)(2,1)S(1)}, bf16[2,1024,512]{2,1,0:T(8,128)(2,1)}, u32[]{:S(2)}) copy-start(bf16[2,1024,512]{2,1,0:T(8,128)(2,1)} %param.10) | copy-start | bytes 6291460
  22.6 4.1 %copy-start.4 = (f32[2,256,256]{2,1,0:T(8,128)}, f32[2,256,256]{2,1,0:T(8,128)S(1)}, u32[]{:S(2)}) copy-start(f32[2,256,256]{2,1,0:T(8,128)S(1)} %get-tuple-element.74) | copy-start | bytes 1572868
  24.4 2.3 copy-start.8
  28.0 21.3 %all-to-all-start = ((bf16[2,256,512]{2,0,1:T(2,128)(2,1)}), bf16[2,256,512]{2,0,1:T(2,128)(2,1)S(1)}, u32[]{:S(2)}, u32[]{:S(2)}) async-start(bf16[2,256,512]{2,0,1:T(2,128)(2,1)} %copy.113), calls=%async_computation | async-start | bytes 1048576 | tf_op jit(solution)/shard_map/all_to_all | solution.py:117
  35.3 0.6 copy-start.16
  35.3 75.3 %copy-start.15 = (f32[2,256]{1,0:T(2,128)}, f32[2,256]{1,0:T(2,128)S(1)}, u32[]{:S(2)}) copy-start(f32[2,256]{1,0:T(2,128)S(1)} %rsqrt.31) | copy-start | bytes 6148
  36.1 0.8 copy-start.6
  58.5 2.2 copy-start.13
  59.9 4.2 %copy-start.10 = (bf16[16,32,1024]{2,1,0:T(8,128)(2,1)}, bf16[16,32,1024]{2,1,0:T(8,128)(2,1)S(1)}, u32[]{:S(2)}) copy-start(bf16[16,32,1024]{2,1,0:T(8,128)(2,1)S(1)} %get-tuple-element.49) | copy-start | bytes 3145732
  60.8 3.4 slice-start.6
  62.3 1.9 slice-start.7
  64.1 2.1 copy-start.7
  67.4 22.2 %all-to-all-start.3 = ((bf16[16,32,512]{2,1,0:T(8,128)(2,1)}), bf16[16,32,512]{2,1,0:T(8,128)(2,1)}, u32[]{:S(2)}, u32[]{:S(2)}) async-start(bf16[16,32,512]{2,1,0:T(8,128)(2,1)} %fusion.56), calls=%async_computation.3 | async-start | bytes 1048576 | tf_op jit(solution)/shard_map/all_to_all | solution.py:128
  82.4 19.0 %copy-start.5 = (f32[2,256,256]{2,1,0:T(8,128)S(1)}, f32[2,256,256]{2,1,0:T(8,128)}, u32[]{:S(2)}) copy-start(f32[2,256,256]{2,1,0:T(8,128)} %copy-done.4) | copy-start | bytes 1572868
  89.6 214.4 %all-to-all-start.1 = ((bf16[16,32,512]{2,1,0:T(8,128)(2,1)}), bf16[16,32,512]{2,1,0:T(8,128)(2,1)}, u32[]{:S(2)}, u32[]{:S(2)}) async-start(bf16[16,32,512]{2,1,0:T(8,128)(2,1)} %fusion.28), calls=%async_computation.1 | async-start | bytes 1048576 | tf_op jit(solution)/shard_map/all_to_all | solution.py:121
  98.5 4.9 %slice-start = ((s8[4456448]{0:T(1024)(128)(4,1)}), s8[4194304]{0:T(1024)(128)(4,1)S(1)}, s32[]{:S(2)}) async-start(s8[4456448]{0:T(1024)(128)(4,1)} %bitcast.162), calls=%async_computation.4 | async-start | bytes 8388608
  98.5 4.9 %slice-start.1 = ((s8[4456448]{0:T(1024)(128)(4,1)}), s8[262144]{0:T(1024)(128)(4,1)S(1)}, s32[]{:S(2)}) async-start(s8[4456448]{0:T(1024)(128)(4,1)} %bitcast.162), calls=%async_computation.5 | async-start | bytes 524288
  103.5 1.7 copy-start.9
  103.5 2.4 copy-start.1
  103.5 5.1 %slice-start.4 = ((s8[4456448]{0:T(1024)(128)(4,1)}), s8[4194304]{0:T(1024)(128)(4,1)S(1)}, s32[]{:S(2)}) async-start(s8[4456448]{0:T(1024)(128)(4,1)} %bitcast.178), calls=%async_computation.8 | async-start | bytes 8388608
  105.2 3.4 slice-start.5
  106.0 6.2 %slice-start.2 = ((s8[4456448]{0:T(1024)(128)(4,1)}), s8[4194304]{0:T(1024)(128)(4,1)S(1)}, s32[]{:S(2)}) async-start(s8[4456448]{0:T(1024)(128)(4,1)} %bitcast.164), calls=%async_computation.6 | async-start | bytes 8388608
  108.6 2.0 copy-start.3
  108.6 3.5 %slice-start.3 = ((s8[4456448]{0:T(1024)(128)(4,1)}), s8[262144]{0:T(1024)(128)(4,1)S(1)}, s32[]{:S(2)}) async-start(s8[4456448]{0:T(1024)(128)(4,1)} %bitcast.164), calls=%async_computation.7 | async-start | bytes 524288
  304.0 6.0 %copy-start.11 = (f32[2,256,512]{2,1,0:T(8,128)S(1)}, f32[2,256,512]{2,1,0:T(8,128)}, u32[]{:S(2)}) copy-start(f32[2,256,512]{2,1,0:T(8,128)} %get-tuple-element.75) | copy-start | bytes 3145732
where the time goes:
time: 348 us; the launch traced here: 347 us
  blocking collectives  216 us (62%)
  matrix products  41.1 us (12%)
  starting transfers between devices  32.9 us (9%)
  other arithmetic  22 us (6%)
  waiting for transfers between devices  17.7 us (5%)
  local copies, waits for them, and re-layouts  15.8 us (5%)
    unnamed x1, blocking collectives  164 us
    psum x5, blocking collectives, over_axes(): return functools.reduce(lax.psum, axes, x)  35.3 us
    all_gather x1, blocking collectives, one_gather(): lines, at, gathered = (lax.all_gather(ravelled, axis), 0, [])  17.1 us
    dot_general x4, matrix products, against(): lax.dot_general(values, weight, (((values.ndim - 1,), (1,)), ((), ())), p...  11.6 us
    all_to_all x1, waiting for transfers between devices, on_device(): lax.all_to_all(first, SEQ, split_axis=1, concat_axis=0, tiled=True)  10.5 us
    all_to_all x1, starting transfers between devices, on_device(): lax.all_to_all(cotangent.reshape(block_count, BLOCK, width), SEQ, split_a...  9.95 us
    dot_general x4, matrix products, rows_product(): lax.dot_general(left_rows, right_rows, (((0,), (0,)), ((), ())), preferre...  9.3 us
    dot_general x2, matrix products, unit_forward(): projected = jnp.dot(hidden, weight_in, preferred_element_type=jnp.float32)  8.71 us
  transfers between devices with their start and end apart: 4, of which 2 were waited for; matrix products, arithmetic and copies ran while one was open for 14% of the time, Pallas kernels for 0%

commit v1 on v0

--- a/solution.py
+++ b/solution.py
@@ -4,6 +4,8 @@
 import jax
 import jax.numpy as jnp
 from jax import lax
+from jax.experimental import pallas as pl
+from jax.experimental.pallas import tpu as pltpu
 from jax.sharding import Mesh
 from jax.sharding import PartitionSpec as P
 
@@ -77,6 +79,393 @@
     )
 
 
+MESH = pl.DeviceIdType.MESH
+NT = 25
+HALVES = ((0, 13), (13, 12))
+
+
+class Links:
+    def __init__(self, send, recv):
+        self.send, self.recv, self.used, self.open = send, recv, 0, []
+        self.x, self.y, self.zl = (lax.axis_index(a) for a in DP)
+        self.zh, self.c = (lax.axis_index(a) for a in SEQ)
+
+    def take(self, count=1):
+        at = self.used
+        self.used += count
+        return at
+
+    def at(self, x=None, y=None, zl=None, zh=None, c=None):
+        return (
+            self.x if x is None else x,
+            self.y if y is None else y,
+            self.zl if zl is None else zl,
+            self.zh if zh is None else zh,
+            self.c if c is None else c,
+        )
+
+    def copy(self, src, dst, target, sem, recv_sem=None):
+        return pltpu.make_async_remote_copy(
+            src_ref=src,
+            dst_ref=dst,
+            send_sem=self.send.at[sem],
+            recv_sem=self.recv.at[sem if recv_sem is None else recv_sem],
+            device_id=target,
+            device_id_type=MESH,
+        )
+
+    def start(self, src, dst, target, sem):
+        op = self.copy(src, dst, target, sem)
+        op.start()
+        self.open.append(op)
+        return op
+
+    def drain(self):
+        for op in self.open:
+            if callable(op):
+                op()
+            else:
+                op.wait_send()
+        self.open = []
+
+
+def mod4(v):
+    return lax.rem(v + 4, 4)
+
+
+def barrier(k):
+    sem = pltpu.get_barrier_semaphore()
+    targets = [k.at(x=mod4(k.x + d)) for d in (1, 2, 3)]
+    targets += [k.at(y=mod4(k.y + d)) for d in (1, 2, 3)]
+    for dl in (0, 1):
+        for dh in range(4):
+            for dc in (0, 1):
+                if dl or dh or dc:
+                    targets.append(
+                        k.at(zl=lax.rem(k.zl + dl, 2), zh=mod4(k.zh + dh), c=lax.rem(k.c + dc, 2))
+                    )
+    for target in targets:
+        pl.semaphore_signal(sem, inc=1, device_id=target, device_id_type=MESH)
+    pl.semaphore_wait(sem, len(targets))
+
+
+def small_sum(k, buf, value_ref, out_ref):
+    f32_pair, f32_x, f32_y, f32_z = 0, 1, 5, 9
+    sems = {}
+
+    def pair():
+        sems["p"] = k.take()
+        k.start(value_ref, buf.at[f32_pair], k.at(c=1 - k.c), sems["p"])
+
+    def x():
+        k.copy(value_ref, buf.at[f32_pair], k.at(c=1 - k.c), sems["p"]).wait_recv()
+        buf[f32_x + k.x] = value_ref[...] + buf[f32_pair]
+        sems["x"] = k.take(3)
+        for d in (1, 2, 3):
+            src = buf.at[f32_x + k.x]
+            k.start(src, src, k.at(x=mod4(k.x + d)), sems["x"] + d - 1)
+
+    def y():
+        for d in (1, 2, 3):
+            slot = buf.at[f32_x + mod4(k.x - d)]
+            k.copy(slot, slot, k.at(x=mod4(k.x - d)), sems["x"] + d - 1).wait_recv()
+        buf[f32_y + k.y] = (buf[f32_x] + buf[f32_x + 1]) + (buf[f32_x + 2] + buf[f32_x + 3])
+        sems["y"] = k.take(3)
+        for d in (1, 2, 3):
+            src = buf.at[f32_y + k.y]
+            k.start(src, src, k.at(y=mod4(k.y + d)), sems["y"] + d - 1)
+
+    def z():
+        for d in (1, 2, 3):
+            slot = buf.at[f32_y + mod4(k.y - d)]
+            k.copy(slot, slot, k.at(y=mod4(k.y - d)), sems["y"] + d - 1).wait_recv()
+        me = 2 * k.zh + k.zl
+        buf[f32_z + me] = (buf[f32_y] + buf[f32_y + 1]) + (buf[f32_y + 2] + buf[f32_y + 3])
+        sems["z"] = k.take(7)
+        for d in range(1, 8):
+            to = lax.rem(me + d, 8)
+            src = buf.at[f32_z + me]
+            k.start(src, src, k.at(zh=to // 2, zl=lax.rem(to, 2)), sems["z"] + d - 1)
+
+    def end():
+        me = 2 * k.zh + k.zl
+        for d in range(1, 8):
+            frm = lax.rem(me + 8 - d, 8)
+            slot = buf.at[f32_z + frm]
+            k.copy(slot, slot, k.at(zh=frm // 2, zl=lax.rem(frm, 2)), sems["z"] + d - 1).wait_recv()
+        parts = [buf[f32_z + i] for i in range(8)]
+        while len(parts) > 1:
+            parts = [a + b for a, b in zip(parts[::2], parts[1::2])]
+        out_ref[...] = parts[0]
+
+    return [pair, x, y, z, end]
+
+
+def sum_stages(k, grads, paired, first_in, second_in, z_in, gathered):
+    sems = {}
+    me = (k.x, k.y)
+
+    def to_axis(half, step, delta):
+        along = (half + step) % 2
+        return k.at(x=mod4(k.x + delta)) if along == 0 else k.at(y=mod4(k.y + delta))
+
+    def view(half, step, delta, part):
+        t0, n = HALVES[half]
+        along = (half + step) % 2
+        dest = mod4(me[along] + delta)
+        if step == 0:
+            sub = pl.ds(0, 4) if part is None else pl.ds(2 * part, 2)
+            return (
+                paired.at[dest, sub, t0 : t0 + n]
+                if along == 0
+                else paired.at[sub, dest, t0 : t0 + n]
+            )
+        cut = (n + 1) // 2
+        lo, hi = {None: (0, n), 0: (0, cut), 1: (cut, n)}[part]
+        return (
+            paired.at[dest, k.y, t0 + lo : t0 + hi]
+            if along == 0
+            else paired.at[k.x, dest, t0 + lo : t0 + hi]
+        )
+
+    def inbox(half, step, direction, part):
+        n = HALVES[half][1]
+        one = first_in[half] if step == 0 else second_in[half]
+        box = one[2 + direction]
+        if part is None:
+            return box
+        if step == 0:
+            return box.at[2 * part : 2 * part + 2]
+        cut = (n + 1) // 2
+        return box.at[0:cut] if part == 0 else box.at[cut:n]
+
+    def outset(half, step):
+        one = first_in[half] if step == 0 else second_in[half]
+        base = sems[half, step] = k.take(6)
+        for direction, delta in ((0, 1), (1, -1)):
+            k.start(
+                view(half, step, 2, direction),
+                one[direction],
+                to_axis(half, step, delta),
+                base + direction,
+            )
+        for direction, delta in ((0, 1), (1, -1)):
+            part = 1 - direction
+            k.start(
+                view(half, step, delta, part),
+                inbox(half, step, direction, part),
+                to_axis(half, step, delta),
+                base + 2 + direction,
+            )
+
+    def relay(half, step):
+        one = first_in[half] if step == 0 else second_in[half]
+        base = sems[half, step]
+        for direction, delta in ((0, 1), (1, -1)):
+            k.copy(
+                one[direction], one[direction], to_axis(half, step, -delta), base + direction
+            ).wait_recv()
+            target = view(half, step, delta, direction)
+            target[...] = target[...] + one[direction][...]
+            k.start(
+                target,
+                inbox(half, step, direction, direction),
+                to_axis(half, step, delta),
+                base + 4 + direction,
+            )
+
+    def collect(half, step):
+        base = sems[half, step]
+        for direction, delta in ((0, 1), (1, -1)):
+            for at, part in ((2, 1 - direction), (4, direction)):
+                box = inbox(half, step, direction, part)
+                k.copy(box, box, to_axis(half, step, -delta), base + at + direction).wait_recv()
+        own = view(half, step, 0, None)
+        f32 = jnp.float32
+        own[...] = (
+            own[...].astype(f32)
+            + (inbox(half, step, 0, None)[...].astype(f32) + inbox(half, step, 1, None)[...].astype(f32))
+        ).astype(jnp.bfloat16)
+
+    def pair_out():
+        sems["pair"] = k.take()
+        k.start(grads.at[:, :, 1 - k.c], paired, k.at(c=1 - k.c), sems["pair"])
+
+    def pair_in():
+        k.copy(paired, paired, k.at(c=1 - k.c), sems["pair"]).wait_recv()
+
+        @pl.loop(0, 4)
+        def _(i):
+            paired[i] = paired[i] + grads[i, :, k.c]
+
+        for half in (0, 1):
+            outset(half, 0)
+
+    def relay_0():
+        for half in (0, 1):
+            relay(half, 0)
+
+    def turn():
+        for half in (0, 1):
+            collect(half, 0)
+            outset(half, 1)
+
+    def relay_1():
+        for half in (0, 1):
+            relay(half, 1)
+
+    def z_out():
+        for half in (0, 1):
+            collect(half, 1)
+        base = sems["z"] = k.take(8)
+        spot = 2 * k.zh + k.zl
+        for q in range(4):
+            for e in range(2):
+                piece = 3 * (2 * q + e)
+                source = paired.at[k.x, k.y, piece : piece + 4]
+                mine = (k.zh == q) & (k.c == e) & (k.zl == k.c)
+                op = pltpu.make_async_remote_copy(
+                    src_ref=source,
+                    dst_ref=z_in.at[spot],
+                    send_sem=k.send.at[base + 2 * q + e],
+                    recv_sem=k.recv.at[base + spot],
+                    device_id=k.at(zl=k.c, zh=q, c=e),
+                    device_id_type=MESH,
+                )
+
+                @pl.when(jnp.logical_not(mine))
+                def _():
+                    op.start()
+
+                @pl.when(mine)
+                def _():
+                    z_in[spot] = source[...]
+
+                def done(op=op, mine=mine):
+                    @pl.when(jnp.logical_not(mine))
+                    def _():
+                        op.wait_send()
+
+                k.open.append(done)
+
+    def z_in_sum():
+        base = sems["z"]
+        spot = 2 * k.zh + k.zl
+        for slot in range(8):
+            mine = (spot == slot) & (k.zl == k.c)
+
+            @pl.when(jnp.logical_not(mine))
+            def _():
+                box = z_in.at[slot]
+                k.copy(box, box, k.at(zh=slot // 2, zl=slot % 2, c=k.zl), base + slot).wait_recv()
+
+        parts = [z_in[i].astype(jnp.float32) for i in range(8)]
+        while len(parts) > 1:
+            parts = [a + b for a, b in zip(parts[::2], parts[1::2])]
+        p = 2 * k.zh + k.c
+        gathered[p] = parts[0].astype(jnp.bfloat16)
+        base = sems["g"] = k.take(7)
+        for d in range(1, 8):
+            to = lax.rem(p + d, 8)
+            box = gathered.at[p]
+            k.start(box, box, k.at(zh=to // 2, c=lax.rem(to, 2)), base + d - 1)
+
+    def gather():
+        p = 2 * k.zh + k.c
+        for d in range(1, 8):
+            frm = lax.rem(p + 8 - d, 8)
+            box = gathered.at[frm]
+            k.copy(box, box, k.at(zh=frm // 2, c=lax.rem(frm, 2)), sems["g"] + d - 1).wait_recv()
+
+    return [pair_out, pair_in, relay_0, turn, relay_1, z_out, z_in_sum, gather]
+
+
+def write_shard(gathered, grad_in_ref, grad_out_ref, scaling):
+    for tile in range(NT):
+        p = min(tile // 3, 7)
+        values = gathered[p, tile - 3 * p].astype(jnp.float32) * scaling
+        if tile < 17:
+            grad_in_ref[:, 128 * tile : 128 * tile + 128] = values
+        else:
+            column, half = (tile - 17) // 2, (tile - 17) % 2
+            grad_out_ref[16 * half : 16 * half + 16, 128 * column : 128 * column + 128] = values
+
+
+def sum_scratch():
+    bf16 = jnp.bfloat16
+    shapes = [pltpu.VMEM((4, 4, NT, 16, 128), bf16)]
+    for _, n in HALVES:
+        shapes += [pltpu.VMEM((2, n, 16, 128), bf16)] * 2 + [pltpu.VMEM((4, n, 16, 128), bf16)] * 2
+    for _, n in HALVES:
+        cut = (n + 1) // 2
+        shapes += [pltpu.VMEM((cut, 16, 128), bf16), pltpu.VMEM((n - cut, 16, 128), bf16)]
+        shapes += [pltpu.VMEM((n, 16, 128), bf16)] * 2
+    shapes += [pltpu.VMEM((8, 4, 16, 128), bf16), pltpu.VMEM((8, 4, 16, 128), bf16)]
+    shapes += [pltpu.VMEM((17, 8, 128), jnp.float32)]
+    return shapes
+
+
+def sum_refs(refs):
+    paired, refs = refs[0], refs[1:]
+    first = (refs[0:4], refs[4:8])
+    second = (refs[8:12], refs[12:16])
+    return (paired, first, second, refs[16], refs[17]), refs[18]
+
+
+SEMS = 160
+
+
+def reduce_kernel(scaling, g_ref, s_ref, in_ref, out_ref, small_ref, *scratch):
+    send, recv = scratch[-2:]
+    k = Links(send, recv)
+    barrier(k)
+    stages = []
+    ends = []
+    for unit in (1, 0):
+        main, buf = sum_refs(scratch[20 * unit : 20 * unit + 20])
+        stages.append(sum_stages(k, g_ref.at[unit], *main))
+        stages.append(small_sum(k, buf, s_ref.at[unit], small_ref.at[unit]))
+        ends.append((main[-1], unit))
+    for step in range(8):
+        for group in stages:
+            if step < len(group):
+                group[step]()
+    for gathered, unit in ends:
+        write_shard(gathered, in_ref.at[unit], out_ref.at[unit], scaling)
+    small_ref[...] = small_ref[...] * scaling
+    k.drain()
+
+
+def reduced(grads, smalls, scaling):
+    vmem = pl.BlockSpec(memory_space=pltpu.VMEM)
+    return pl.pallas_call(
+        functools.partial(reduce_kernel, scaling),
+        out_shape=(
+            jax.ShapeDtypeStruct((2, 16, 2176), jnp.float32),
+            jax.ShapeDtypeStruct((2, 32, 512), jnp.float32),
+            jax.ShapeDtypeStruct((2, 8, 128), jnp.float32),
+        ),
+        in_specs=[vmem, vmem],
+        out_specs=(vmem, vmem, vmem),
+        scratch_shapes=sum_scratch()
+        + sum_scratch()
+        + [pltpu.SemaphoreType.DMA((SEMS,)), pltpu.SemaphoreType.DMA((SEMS,))],
+        compiler_params=pltpu.CompilerParams(
+            collective_id=0, has_side_effects=True, vmem_limit_bytes=48 * 1024 * 1024
+        ),
+    )(grads, smalls)
+
+
+def as_tiles(grad_in, grad_out):
+    left = grad_in.astype(jnp.bfloat16).reshape(4, 4, 2, 16, 17, 128).transpose(0, 1, 2, 4, 3, 5)
+    right = grad_out.astype(jnp.bfloat16).reshape(4, 4, 2, 2, 16, 4, 128).transpose(0, 1, 2, 5, 3, 4, 6)
+    return jnp.concatenate([left, right.reshape(4, 4, 2, 8, 16, 128)], axis=3)
+
+
+def small_tile(gain, scale):
+    return jnp.concatenate([gain.reshape(4, 128), scale.reshape(2, 128), jnp.zeros((2, 128), jnp.float32)])
+
+
 def unit_forward(inputs_now, weight_in, scale_pair, weight_out, gain_row, attend_axis):
     hidden = normed(inputs_now.astype(jnp.float32), gain_row).astype(jnp.bfloat16)
     projected = jnp.dot(hidden, weight_in, preferred_element_type=jnp.float32)
@@ -129,30 +518,16 @@
     back_frames, in_early, out_early, gain_early, scale_early = unit_backward(
         blocked, back_first, weight_in[0], qk_scales[0], weight_out[0], gains[0], saved_first, 1
     )
-    grad_in = jnp.stack([in_early, in_late]) * scaling
-    grad_out = jnp.stack([out_early, out_late]) * scaling
-    grad_gains = jnp.stack([gain_early, gain_late]) * scaling
-    grad_scales = jnp.stack([scale_early, scale_late]) * scaling
-    shares = (
-        lax.psum_scatter(grad_in, DP_SEQ, scatter_dimension=1, tiled=True),
-        lax.psum_scatter(grad_out, DP_SEQ, scatter_dimension=1, tiled=True),
-    )
-    summed = tuple(
-        (
-            part.astype(jnp.float32)
-            for part in one_gather(
-                (shares[0].astype(jnp.bfloat16), shares[1].astype(jnp.bfloat16)), SEQ, (1, 1)
-            )
-        )
-    )
-    small = (over_axes(grad_gains, DP_SEQ), over_axes(grad_scales, DP_SEQ))
+    grads = jnp.stack([as_tiles(in_early, out_early), as_tiles(in_late, out_late)])
+    smalls = jnp.stack([small_tile(gain_early, scale_early), small_tile(gain_late, scale_late)])
+    grad_in, grad_out, small = reduced(grads, smalls, scaling)
     return (
         result.reshape(frames.shape),
         back_frames.reshape(frames.shape),
-        summed[0],
-        summed[1],
-        small[0],
-        small[1],
+        grad_in,
+        grad_out,
+        small[:, :4].reshape(2, 512),
+        small[:, 4:6],
     )
 
 

time: 348 us -> 199 us (0.57)
  blocking collectives: 216 us -> 0 us
  Pallas kernels: 0 us -> 54.3 us
  local copies, waits for them, and re-layouts: 15.8 us -> 30.6 us
  other arithmetic: 22 us -> 18.5 us
    unnamed x1 -> x0, blocking collectives: 164 us -> none
    pallas_call x0 -> x1, Pallas kernels: none -> 54.3 us  [reduced(): pl.pallas_call(functools.partial(reduce_kernel, scaling), out_shape=(jax....]
    psum x5 -> x0, blocking collectives: 35.3 us -> none  [over_axes(): return functools.reduce(lax.psum, axes, x)]
    all_gather x1 -> x0, blocking collectives: 17.1 us -> none  [one_gather(): lines, at, gathered = (lax.all_gather(ravelled, axis), 0, [])]
    reshape x1 -> x8, local copies, waits for them, and re-layouts: 0.04 us -> 16.2 us  [the longest x4 11.1 us: as_tiles(): grad_in.astype(jnp.bfloat16).reshape(4, 4, 2, 16, 17, 128)]
    mul x4 -> x0, other arithmetic: 7.58 us -> none  [the longest x1 4.21 us: on_device(): grad_in = jnp.stack([in_early, in_late]) * scaling]
    all_to_all x1, waiting for transfers between devices: 7.23 us -> 0.01 us  [on_device(): lax.all_to_all(back_pos, SEQ, split_axis=0, concat_axis=1, tiled=True)]
    all_to_all x1, waiting for transfers between devices: 0.01 us -> 6.59 us  [on_device(): lax.all_to_all(cotangent.reshape(block_count, BLOCK, width), SEQ, split_a...]
  transfers between devices with their start and end apart: 4 -> 4, of which waited for: 2 -> 2; matrix products, arithmetic and copies ran while one was open for 14% -> 28% of each run, Pallas kernels for 0% -> 27%
where the time goes in v1:
time: 199 us; the launch traced here: 198 us
  Pallas kernels  54.3 us (27%)
  matrix products  42.5 us (21%)
  starting transfers between devices  32.3 us (16%)
  local copies, waits for them, and re-layouts  30.6 us (15%)
  other arithmetic  18.5 us (9%)
  waiting for transfers between devices  18.5 us (9%)
    pallas_call x1, Pallas kernels, reduced(): pl.pallas_call(functools.partial(reduce_kernel, scaling), out_shape=(jax....  54.3 us
    dot_general x2, matrix products, unit_forward(): projected = jnp.dot(hidden, weight_in, preferred_element_type=jnp.float32)  12.1 us
    all_to_all x1, waiting for transfers between devices, on_device(): lax.all_to_all(first, SEQ, split_axis=1, concat_axis=0, tiled=True)  11.9 us
    reshape x4, local copies, waits for them, and re-layouts, as_tiles(): grad_in.astype(jnp.bfloat16).reshape(4, 4, 2, 16, 17, 128)  11.1 us
    dot_general x4, matrix products, rows_product(): lax.dot_general(left_rows, right_rows, (((0,), (0,)), ((), ())), preferre...  10.1 us
    all_to_all x1, starting transfers between devices, on_device(): lax.all_to_all(first, SEQ, split_axis=1, concat_axis=0, tiled=True)  9.95 us
    dot_general x4, matrix products, against(): lax.dot_general(values, weight, (((values.ndim - 1,), (1,)), ((), ())), p...  9.13 us
    all_to_all x1, starting transfers between devices, on_device(): lax.all_to_all(back_pos, SEQ, split_axis=0, concat_axis=1, tiled=True)  7.76 us
  transfers between devices with their start and end apart: 4, of which 2 were waited for; matrix products, arithmetic and copies ran while one was open for 28% of the time, Pallas kernels for 27%

profile of v1, /device:TPU:1, one launch (start us, length us, event | category | flops | bytes accessed | tf_op | source)
XLA Modules:
  0.0 198.0 jit_solution(9935080477962394675)
XLA Ops:
  4.6 5.4 %fusion.9 = (f32[2,256,2176]{2,1,0:T(8,128)S(1)}, f32[2,256,2176]{2,1,0:T(8,128)}) fusion(bf16[2,256,512]{2,1,0:T(8,128)(2,1)S(1)} %bitcast.196, bf16[2,512,2176]{2,1,0:T(8,128)(2,1)} %param.8), kind=kOutput, calls=%fused_computation.16 | convolution fusion | flops 1145307136 | bytes 11665408 | tf_op jit(solution)/shard_map/dot_general | solution.py:471
  10.3 1.8 multiply_convert_fusion
  14.4 1.3 copy.119
  15.7 10.0 %all-to-all-start = ((bf16[2,256,512]{2,0,1:T(2,128)(2,1)}), bf16[2,256,512]{2,0,1:T(2,128)(2,1)S(1)}, u32[]{:S(2)}, u32[]{:S(2)}) async-start(bf16[2,256,512]{2,0,1:T(2,128)(2,1)} %copy.119), calls=%async_computation | async-start | bytes 1048576 | tf_op jit(solution)/shard_map/all_to_all | solution.py:506
  25.7 1.3 copy.126
  27.8 11.9 %all-to-all-done = bf16[2,256,512]{2,0,1:T(2,128)(2,1)S(1)} async-done(((bf16[2,256,512]{2,0,1:T(2,128)(2,1)}), bf16[2,256,512]{2,0,1:T(2,128)(2,1)S(1)}, u32[]{:S(2)}, u32[]{:S(2)}) %all-to-all-start) | async-done | bytes 524320 | tf_op jit(solution)/shard_map/all_to_all | solution.py:506
  39.8 7.4 %all-to-all-start.2 = ((bf16[2,256,512]{2,0,1:T(2,128)(2,1)}), bf16[2,256,512]{2,0,1:T(2,128)(2,1)S(1)}, u32[]{:S(2)}, u32[]{:S(2)}) async-start(bf16[2,256,512]{2,0,1:T(2,128)(2,1)} %copy.126), calls=%async_computation.2 | async-start | bytes 1048576 | tf_op jit(solution)/shard_map/all_to_all | solution.py:511
  48.0 6.7 %fusion.8 = (f32[16,32,2176]{2,1,0:T(8,128)}, f32[16,32,2176]{2,1,0:T(8,128)}) fusion(bf16[16,32,512]{2,1,0:T(8,128)(2,1)S(1)} %bitcast.195, bf16[2,512,2176]{2,1,0:T(8,128)(2,1)} %param.8), kind=kOutput, calls=%fused_computation.14 | convolution fusion | flops 1145307136 | bytes 11665408 | tf_op jit(solution)/shard_map/dot_general | solution.py:471
  54.8 6.6 %all-to-all-done.2 = bf16[2,256,512]{2,0,1:T(2,128)(2,1)S(1)} async-done(((bf16[2,256,512]{2,0,1:T(2,128)(2,1)}), bf16[2,256,512]{2,0,1:T(2,128)(2,1)S(1)}, u32[]{:S(2)}, u32[]{:S(2)}) %all-to-all-start.2) | async-done | bytes 524320 | tf_op jit(solution)/shard_map/all_to_all | solution.py:511
  61.5 2.2 %convolution_convert_fusion.4 = bf16[16,32,1024]{2,1,0:T(8,128)(2,1)S(1)} fusion(bf16[16,32,512]{2,1,0:T(8,128)(2,1)S(1)} %bitcast.189, bf16[2,1024,512]{2,1,0:T(8,128)(2,1)} %param.10), kind=kOutput, calls=%fused_computation.54 | convolution fusion | flops 537395200 | bytes 2621440 | tf_op jit(solution)/shard_map/dot_general | solution.py:77
  68.9 2.3 %convert_multiply_fusion.2 = (f32[16,32,1024]{2,1,0:T(8,128)S(1)}, bf16[16,32,1024]{2,1,0:T(8,128)(2,1)}) fusion(bf16[16,32,1024]{2,1,0:T(8,128)(2,1)S(1)} %convolution_convert_fusion.4, f32[32,1024,16]{1,2,0:T(8,128)S(1)} %fusion.70, f32[16,32,2176]{2,1,0:T(8,128)S(1)} %copy-done.5), kind=kLoop, calls=%fused_computation.21 | loop fusion | flops 2097152 | bytes 8388608 | tf_op jit(solution)/shard_map/transpose(jvp())/mul | solution.py:65
  72.2 1.9 fusion.4
  74.4 2.1 %multiply_reduce_fusion = (f32[512]{0:T(512)}, f32[16,32]{1,0:T(8,128)S(1)}, f32[16,32,512]{2,1,0:T(8,128)S(1)}) fusion(f32[16,32]{1,0:T(8,128)S(1)} %rsqrt.30, f32[2,8,32,512]{3,2,0,1:T(8,128)S(1)} %copy.120, f32[16,32,512]{2,1,0:T(8,128)S(1)} %bitcast.185, f32[512]{0:T(512)S(1)} %bitcast.205, bf16[16,32,2176]{2,1,0:T(8,128)(2,1)S(1)} %fusion.4, ...), kind=kOutput, calls=%fused_computation.92 | convolution fusion | flops 1142422528 | bytes 7616512 | tf_op jit(solution)/shard_map/dot_general | solution.py:77
  77.6 7.8 %all-to-all-start.3 = ((bf16[16,32,512]{2,1,0:T(8,128)(2,1)}), bf16[16,32,512]{2,1,0:T(8,128)(2,1)}, u32[]{:S(2)}, u32[]{:S(2)}) async-start(bf16[16,32,512]{2,1,0:T(8,128)(2,1)} %fusion.58), calls=%async_computation.3 | async-start | bytes 1048576 | tf_op jit(solution)/shard_map/all_to_all | solution.py:517
  85.4 4.6 %fusion.1 = bf16[512,2176]{1,0:T(8,128)(2,1)} fusion(bf16[16,32,2176]{2,1,0:T(8,128)(2,1)} %copy-done.15, f32[16,32,512]{2,1,0:T(8,128)S(1)} %bitcast.186, f32[16,32]{1,0:T(8,128)S(1)} %rsqrt.30, f32[512]{0:T(512)S(1)} %bitcast.207), kind=kOutput, calls=%fused_computation.6 | convolution fusion | flops 1142751232 | bytes 5509120 | tf_op jit(solution)/shard_map/dot_general | solution.py:71
  90.0 3.8 %reshape.172 = bf16[4,4,2,16,17,128]{5,4,3,2,1,0:T(8,128)(2,1)S(1)} reshape(bf16[512,2176]{1,0:T(8,128)(2,1)} %fusion.1) | data formatting | bytes 4456448 | tf_op jit(solution)/shard_map/reshape | solution.py:460
  93.8 1.8 copy.206
  97.9 3.2 %fusion.30 = bf16[16,32,512]{2,1,0:T(8,128)(2,1)} fusion(f32[16,32,512]{2,1,0:T(8,128)S(1)} %bitcast.187, bf16[16,32,1024]{2,1,0:T(8,128)(2,1)} %get-tuple-element.25, bf16[2,1024,512]{2,1,0:T(8,128)(2,1)} %param.10), kind=kOutput, calls=%fused_computation.59 | convolution fusion | flops 537395200 | bytes 3670016 | tf_op jit(solution)/shard_map/dot_general | solution.py:475
  101.1 7.2 %all-to-all-start.1 = ((bf16[16,32,512]{2,1,0:T(8,128)(2,1)}), bf16[16,32,512]{2,1,0:T(8,128)(2,1)}, u32[]{:S(2)}, u32[]{:S(2)}) async-start(bf16[16,32,512]{2,1,0:T(8,128)(2,1)} %fusion.30), calls=%async_computation.1 | async-start | bytes 1048576 | tf_op jit(solution)/shard_map/all_to_all | solution.py:510
  109.6 2.4 %convert_multiply_fusion = (f32[2,256,1024]{2,1,0:T(8,128)S(1)}, bf16[2,256,1024]{2,1,0:T(8,128)(2,1)S(1)}) fusion(f32[2,256,1024]{2,1,0:T(8,128)S(1)} %copy-done.4, bf16[2,256,512]{2,1,0:T(8,128)(2,1)S(1)} %bitcast.176, bf16[2,1024,512]{2,1,0:T(8,128)(2,1)} %param.10), kind=kOutput, calls=%fused_computation.19 | convolution fusion | flops 538443776 | bytes 6815744 | tf_op jit(solution)/shard_map/dot_general | solution.py:77
  114.3 1.9 fusion.7
  116.3 2.5 %multiply_reduce_fusion.1 = (f32[512]{0:T(512)S(1)}, f32[2,256]{1,0:T(2,128)S(1)}, f32[2,256,512]{2,1,0:T(8,128)}) fusion(f32[2,256]{1,0:T(2,128)S(1)} %rsqrt.31, f32[512]{0:T(512)S(1)} %bitcast.201, bf16[2,256,2176]{2,1,0:T(8,128)(2,1)S(1)} %fusion.7, bf16[2,512,2176]{2,1,0:T(8,128)(2,1)S(1)} %bitcast.218, bf16[2,256,512]{2,1,0:T(8,128)(2,1)S(1)} %bitcast.173), kind=kOutput, calls=%fused_computation.93 | convolution fusion | flops 1142684672 | bytes 6037504 | tf_op jit(solution)/shard_map/dot_general | solution.py:77
  118.7 2.9 %fusion = bf16[512,2176]{1,0:T(8,128)(2,1)} fusion(bf16[2,256,2176]{2,1,0:T(8,128)(2,1)S(1)} %fusion.7, f32[2,256]{1,0:T(2,128)S(1)} %rsqrt.31, f32[512]{0:T(512)S(1)} %bitcast.202, bf16[2,256,512]{2,1,0:T(8,128)(2,1)S(1)} %bitcast.174), kind=kOutput, calls=%fused_computation.5 | convolution fusion | flops 1143013376 | bytes 4984832 | tf_op jit(solution)/shard_map/dot_general | solution.py:71
  121.6 3.8 %reshape.167 = bf16[4,4,2,16,17,128]{5,4,3,2,1,0:T(8,128)(2,1)S(1)} reshape(bf16[512,2176]{1,0:T(8,128)(2,1)} %fusion) | data formatting | bytes 4456448 | tf_op jit(solution)/shard_map/reshape | solution.py:460
  125.4 1.8 copy.207
  127.3 1.8 convolution_convert_fusion.2
  129.1 2.1 %reshape.170 = bf16[4,4,2,2,16,4,128]{6,5,4,3,2,1,0:T(4,128)(2,1)} reshape(bf16[1024,512]{1,0:T(8,128)(2,1)} %convolution_convert_fusion.2) | data formatting | bytes 2097152 | tf_op jit(solution)/shard_map/reshape | solution.py:461
  131.2 1.4 copy.144
  132.7 1.9 maximum_bitcast_fusion
  134.8 3.3 %pad_maximum_fusion.g_ref = bf16[2,4,4,2,25,16,128]{6,5,4,3,2,1,0:T(8,128)(2,1)} fusion(bf16[1,4,4,2,25,16,128]{6,5,4,3,2,1,0:T(8,128)(2,1)S(1)} %get-tuple-element.55, bf16[1,4,4,2,25,16,128]{6,5,4,3,2,1,0:T(8,128)(2,1)S(1)} %get-tuple-element.54), kind=kLoop, calls=%fused_computation.2 | loop fusion | flops 3276800 | bytes 13107200 | tf_op jit(solution)/shard_map/stack | solution.py:521
  138.1 54.3 %shard_map.109 = (f32[2,16,2176]{2,1,0:T(8,128)S(1)}, f32[2,32,512]{2,1,0:T(8,128)S(1)}, f32[2,8,128]{2,1,0:T(8,128)S(1)}) custom-call(bf16[2,4,4,2,25,16,128]{6,5,4,3,2,1,0:T(8,128)(2,1)} %pad_maximum_fusion.g_ref, f32[2,8,128]{2,1,0:T(8,128)S(1)} %pad_maximum_fusion.1.s_ref), custom_call_target="tpu_custom_call" | custom-call | tf_op jit(solution)/shard_map/pallas_call | solution.py:441
  193.6 1.9 copy.125
  (138 shorter events, 25.5 us)
Async XLA Ops:
  3.4 6.6 %copy-start.24 = (f32[128]{0:T(128)}, f32[128]{0:T(128)S(1)}, u32[]{:S(2)}) copy-start(f32[128]{0:T(128)S(1)} %get-tuple-element.36) | copy-start | bytes 1540
  10.0 3.1 %copy-start = (f32[2,256,2176]{2,1,0:T(8,128)}, f32[2,256,2176]{2,1,0:T(8,128)S(1)}, u32[]{:S(2)}) copy-start(f32[2,256,2176]{2,1,0:T(8,128)S(1)} %get-tuple-element.40) | copy-start | bytes 13369348
  10.0 3.1 %copy-start.6 = (bf16[1,512,512]{2,1,0:T(8,128)(2,1)S(1)}, bf16[1,512,512]{2,1,0:T(8,128)(2,1)}, u32[]{:S(2)}) copy-start(bf16[1,512,512]{2,1,0:T(8,128)(2,1)} %param.6) | copy-start | bytes 1572868
  10.0 3.6 %copy-start.23 = (bf16[2,1024,512]{2,1,0:T(8,128)(2,1)S(1)}, bf16[2,1024,512]{2,1,0:T(8,128)(2,1)}, u32[]{:S(2)}) copy-start(bf16[2,1024,512]{2,1,0:T(8,128)(2,1)} %param.10) | copy-start | bytes 6291460
  10.3 4.1 %copy-start.2 = (f32[2,256,256]{2,1,0:T(8,128)}, f32[2,256,256]{2,1,0:T(8,128)S(1)}, u32[]{:S(2)}) copy-start(f32[2,256,256]{2,1,0:T(8,128)S(1)} %get-tuple-element.52) | copy-start | bytes 1572868
  13.1 12.6 %copy-start.22 = (bf16[1,512,512]{2,1,0:T(8,128)(2,1)S(1)}, bf16[1,512,512]{2,1,0:T(8,128)(2,1)}, u32[]{:S(2)}) copy-start(bf16[1,512,512]{2,1,0:T(8,128)(2,1)} %param.7) | copy-start | bytes 1572868
  15.7 24.0 %all-to-all-start = ((bf16[2,256,512]{2,0,1:T(2,128)(2,1)}), bf16[2,256,512]{2,0,1:T(2,128)(2,1)S(1)}, u32[]{:S(2)}, u32[]{:S(2)}) async-start(bf16[2,256,512]{2,0,1:T(2,128)(2,1)} %copy.119), calls=%async_computation | async-start | bytes 1048576 | tf_op jit(solution)/shard_map/all_to_all | solution.py:506
  39.8 21.6 %all-to-all-start.2 = ((bf16[2,256,512]{2,0,1:T(2,128)(2,1)}), bf16[2,256,512]{2,0,1:T(2,128)(2,1)S(1)}, u32[]{:S(2)}, u32[]{:S(2)}) async-start(bf16[2,256,512]{2,0,1:T(2,128)(2,1)} %copy.126), calls=%async_computation.2 | async-start | bytes 1048576 | tf_op jit(solution)/shard_map/all_to_all | solution.py:511
  61.3 2.8 %copy-start.5 = (f32[16,32,2176]{2,1,0:T(8,128)S(1)}, f32[16,32,2176]{2,1,0:T(8,128)}, u32[]{:S(2)}) copy-start(f32[16,32,2176]{2,1,0:T(8,128)} %get-tuple-element.44) | copy-start | bytes 13369348
  61.5 15.0 %copy-start.16 = (bf16[8,2,32,512]{3,2,1,0:T(8,128)(2,1)}, bf16[8,2,32,512]{3,2,1,0:T(8,128)(2,1)S(1)}, u32[]{:S(2)}) copy-start(bf16[8,2,32,512]{3,2,1,0:T(8,128)(2,1)S(1)} %copy.128) | copy-start | bytes 1572868
  68.3 3.9 %slice-start.4 = ((s8[4456448]{0:T(1024)(128)(4,1)}), s8[4194304]{0:T(1024)(128)(4,1)S(1)}, s32[]{:S(2)}) async-start(s8[4456448]{0:T(1024)(128)(4,1)} %bitcast.180), calls=%async_computation.8 | async-start | bytes 8388608
  68.9 3.3 %slice-start.5 = ((s8[4456448]{0:T(1024)(128)(4,1)}), s8[262144]{0:T(1024)(128)(4,1)S(1)}, s32[]{:S(2)}) async-start(s8[4456448]{0:T(1024)(128)(4,1)} %bitcast.180), calls=%async_computation.9 | async-start | bytes 524288
  71.3 2.8 %slice-start.6 = ((s8[4456448]{0:T(1024)(128)(4,1)}), s8[262144]{0:T(1024)(128)(4,1)S(1)}, s32[]{:S(2)}) async-start(s8[4456448]{0:T(1024)(128)(4,1)} %bitcast.215), calls=%async_computation.10 | async-start | bytes 524288
  71.5 14.0 %copy-start.13 = (f32[2,8,32,512]{3,2,0,1:T(8,128)}, f32[2,8,32,512]{3,2,0,1:T(8,128)S(1)}, u32[]{:S(2)}) copy-start(f32[2,8,32,512]{3,2,0,1:T(8,128)S(1)} %copy.120) | copy-start | bytes 3145732
  74.1 2.4 %copy-start.15 = (bf16[16,32,2176]{2,1,0:T(8,128)(2,1)}, bf16[16,32,2176]{2,1,0:T(8,128)(2,1)S(1)}, u32[]{:S(2)}) copy-start(bf16[16,32,2176]{2,1,0:T(8,128)(2,1)S(1)} %fusion.4) | copy-start | bytes 6684676
  77.6 23.4 %all-to-all-start.3 = ((bf16[16,32,512]{2,1,0:T(8,128)(2,1)}), bf16[16,32,512]{2,1,0:T(8,128)(2,1)}, u32[]{:S(2)}, u32[]{:S(2)}) async-start(bf16[16,32,512]{2,1,0:T(8,128)(2,1)} %fusion.58), calls=%async_computation.3 | async-start | bytes 1048576 | tf_op jit(solution)/shard_map/all_to_all | solution.py:517
  95.6 2.3 %copy-start.14 = (f32[2,8,32,512]{3,2,0,1:T(8,128)S(1)}, f32[2,8,32,512]{3,2,0,1:T(8,128)}, u32[]{:S(2)}) copy-start(f32[2,8,32,512]{3,2,0,1:T(8,128)} %copy-done.13) | copy-start | bytes 3145732
  96.6 15.3 %slice-start = ((s8[4456448]{0:T(1024)(128)(4,1)}), s8[262144]{0:T(1024)(128)(4,1)S(1)}, s32[]{:S(2)}) async-start(s8[4456448]{0:T(1024)(128)(4,1)} %bitcast.167), calls=%async_computation.4 | async-start | bytes 524288
  97.9 11.7 %copy-start.4 = (f32[2,256,1024]{2,1,0:T(8,128)S(1)}, f32[2,256,1024]{2,1,0:T(8,128)}, u32[]{:S(2)}) copy-start(f32[2,256,1024]{2,1,0:T(8,128)} %get-tuple-element.43) | copy-start | bytes 6291460
  101.1 92.5 %all-to-all-start.1 = ((bf16[16,32,512]{2,1,0:T(8,128)(2,1)}), bf16[16,32,512]{2,1,0:T(8,128)(2,1)}, u32[]{:S(2)}, u32[]{:S(2)}) async-start(bf16[16,32,512]{2,1,0:T(8,128)(2,1)} %fusion.30), calls=%async_computation.1 | async-start | bytes 1048576 | tf_op jit(solution)/shard_map/all_to_all | solution.py:510
  108.3 3.6 %slice-start.1 = ((s8[4456448]{0:T(1024)(128)(4,1)}), s8[4194304]{0:T(1024)(128)(4,1)S(1)}, s32[]{:S(2)}) async-start(s8[4456448]{0:T(1024)(128)(4,1)} %bitcast.167), calls=%async_computation.5 | async-start | bytes 8388608
  109.5 2.4 %copy-start.9 = (bf16[8,2,32,512]{3,2,0,1:T(8,128)(2,1)}, bf16[8,2,32,512]{3,2,0,1:T(8,128)(2,1)S(1)}, u32[]{:S(2)}) copy-start(bf16[8,2,32,512]{3,2,0,1:T(8,128)(2,1)S(1)} %copy.139) | copy-start | bytes 1572868
  109.6 2.4 %copy-start.3 = (f32[2,256,256]{2,1,0:T(8,128)S(1)}, f32[2,256,256]{2,1,0:T(8,128)}, u32[]{:S(2)}) copy-start(f32[2,256,256]{2,1,0:T(8,128)} %copy-done.2) | copy-start | bytes 1572868
  112.0 2.2 %slice-start.2 = ((s8[4456448]{0:T(1024)(128)(4,1)}), s8[4194304]{0:T(1024)(128)(4,1)S(1)}, s32[]{:S(2)}) async-start(s8[4456448]{0:T(1024)(128)(4,1)} %bitcast.178), calls=%async_computation.6 | async-start | bytes 8388608
  112.5 3.7 %slice-start.8 = ((s8[4456448]{0:T(1024)(128)(4,1)}), s8[4194304]{0:T(1024)(128)(4,1)S(1)}, s32[]{:S(2)}) async-start(s8[4456448]{0:T(1024)(128)(4,1)} %bitcast.217), calls=%async_computation.12 | async-start | bytes 8388608
  127.2 5.4 %copy-start.26 = (f32[128]{0:T(128)S(1)}, f32[128]{0:T(128)}, u32[]{:S(2)}) copy-start(f32[128]{0:T(128)} %get-tuple-element.14) | copy-start | bytes 1540
  127.2 5.4 %copy-start.27 = (f32[128]{0:T(128)S(1)}, f32[128]{0:T(128)}, u32[]{:S(2)}) copy-start(f32[128]{0:T(128)} %get-tuple-element.15) | copy-start | bytes 1540
  127.2 5.4 %copy-start.1 = (bf16[4,4,2,16,17,128]{5,3,4,2,1,0:T(8,128)(2,1)S(1)}, bf16[4,4,2,16,17,128]{5,3,4,2,1,0:T(8,128)(2,1)}, u32[]{:S(2)}) copy-start(bf16[4,4,2,16,17,128]{5,3,4,2,1,0:T(8,128)(2,1)} %copy.206) | copy-start | bytes 6684676
  127.3 5.4 %copy-start.12 = (bf16[4,4,2,2,16,4,128]{6,4,3,5,2,1,0:T(8,128)(2,1)S(1)}, bf16[4,4,2,2,16,4,128]{6,4,3,5,2,1,0:T(8,128)(2,1)}, u32[]{:S(2)}) copy-start(bf16[4,4,2,2,16,4,128]{6,4,3,5,2,1,0:T(8,128)(2,1)} %copy.147) | copy-start | bytes 3145732
  138.1 57.4 %copy-start.8 = (bf16[1,512,512]{2,1,0:T(8,128)(2,1)S(1)}, bf16[1,512,512]{2,1,0:T(8,128)(2,1)}, u32[]{:S(2)}) copy-start(bf16[1,512,512]{2,1,0:T(8,128)(2,1)} %param.6) | copy-start | bytes 1572868
  138.1 57.4 %copy-start.11 = (bf16[8,2,32,512]{3,2,0,1:T(8,128)(2,1)S(1)}, bf16[8,2,32,512]{3,2,0,1:T(8,128)(2,1)}, u32[]{:S(2)}) copy-start(bf16[8,2,32,512]{3,2,0,1:T(8,128)(2,1)} %copy-done.9) | copy-start | bytes 1572868
  138.1 57.4 %copy-start.18 = (f32[2,256,512]{2,1,0:T(8,128)S(1)}, f32[2,256,512]{2,1,0:T(8,128)}, u32[]{:S(2)}) copy-start(f32[2,256,512]{2,1,0:T(8,128)} %get-tuple-element.53) | copy-start | bytes 3145732
  (12 other events, 21.2 us)

commit v2 on v1

v2 whole, which is shorter than its diff:
```python
import functools

import jax
import jax.numpy as jnp
from jax import lax
from jax.experimental import pallas as pl
from jax.experimental.pallas import tpu as pltpu
from jax.sharding import Mesh
from jax.sharding import PartitionSpec as P

DP = ("dp_0", "dp_1", "dp_2")
SEQ = ("seq_0", "seq_1")
D, E, S, BLOCK = 512, 1024, 128, 256
WIDE = 2 * E + S
EPSILON = 1e-06
F32, BF16 = jnp.float32, jnp.bfloat16
NT = 25
IN_TILES, OUT_TILES = (0, 17), (17, 8)
SEMS = 300


MESH = pl.DeviceIdType.MESH


def halves_of(n):
    return ((0, (n + 1) // 2), ((n + 1) // 2, n // 2))


def pieces_of(n):
    return n // 8, n - 7 * (n // 8)


class Links:
    def __init__(self, send, recv):
        self.send, self.recv, self.used, self.open = send, recv, 0, []
        self.x, self.y, self.zl = (lax.axis_index(a) for a in DP)
        self.zh, self.c = (lax.axis_index(a) for a in SEQ)

    def take(self, count=1):
        at = self.used
        self.used += count
        return at

    def at(self, x=None, y=None, zl=None, zh=None, c=None):
        return (
            self.x if x is None else x,
            self.y if y is None else y,
            self.zl if zl is None else zl,
            self.zh if zh is None else zh,
            self.c if c is None else c,
        )

    def copy(self, src, dst, target, sem, recv_sem=None):
        return pltpu.make_async_remote_copy(
            src_ref=src,
            dst_ref=dst,
            send_sem=self.send.at[sem],
            recv_sem=self.recv.at[sem if recv_sem is None else recv_sem],
            device_id=target,
            device_id_type=MESH,
        )

    def start(self, src, dst, target, sem):
        op = self.copy(src, dst, target, sem)
        op.start()
        self.open.append(op)
        return op

    def drain(self):
        for op in self.open:
            if callable(op):
                op()
            else:
                op.wait_send()
        self.open = []


def mod4(v):
    return lax.rem(v + 4, 4)


def barrier(k):
    sem = pltpu.get_barrier_semaphore()
    targets = [k.at(x=mod4(k.x + d)) for d in (1, 2, 3)]
    targets += [k.at(y=mod4(k.y + d)) for d in (1, 2, 3)]
    for dl in (0, 1):
        for dh in range(4):
            for dc in (0, 1):
                if dl or dh or dc:
                    targets.append(
                        k.at(zl=lax.rem(k.zl + dl, 2), zh=mod4(k.zh + dh), c=lax.rem(k.c + dc, 2))
                    )
    for target in targets:
        pl.semaphore_signal(sem, inc=1, device_id=target, device_id_type=MESH)
    pl.semaphore_wait(sem, len(targets))


def small_sum(k, buf, value_ref, out_ref):
    f32_pair, f32_x, f32_y, f32_z = 0, 1, 5, 9
    sems = {}

    def pair():
        sems["p"] = k.take()
        k.start(value_ref, buf.at[f32_pair], k.at(c=1 - k.c), sems["p"])

    def x():
        k.copy(value_ref, buf.at[f32_pair], k.at(c=1 - k.c), sems["p"]).wait_recv()
        buf[f32_x + k.x] = value_ref[...] + buf[f32_pair]
        sems["x"] = k.take(3)
        for d in (1, 2, 3):
            src = buf.at[f32_x + k.x]
            k.start(src, src, k.at(x=mod4(k.x + d)), sems["x"] + d - 1)

    def y():
        for d in (1, 2, 3):
            slot = buf.at[f32_x + mod4(k.x - d)]
            k.copy(slot, slot, k.at(x=mod4(k.x - d)), sems["x"] + d - 1).wait_recv()
        buf[f32_y + k.y] = (buf[f32_x] + buf[f32_x + 1]) + (buf[f32_x + 2] + buf[f32_x + 3])
        sems["y"] = k.take(3)
        for d in (1, 2, 3):
            src = buf.at[f32_y + k.y]
            k.start(src, src, k.at(y=mod4(k.y + d)), sems["y"] + d - 1)

    def z():
        for d in (1, 2, 3):
            slot = buf.at[f32_y + mod4(k.y - d)]
            k.copy(slot, slot, k.at(y=mod4(k.y - d)), sems["y"] + d - 1).wait_recv()
        me = 2 * k.zh + k.zl
        buf[f32_z + me] = (buf[f32_y] + buf[f32_y + 1]) + (buf[f32_y + 2] + buf[f32_y + 3])
        sems["z"] = k.take(7)
        for d in range(1, 8):
            to = lax.rem(me + d, 8)
            src = buf.at[f32_z + me]
            k.start(src, src, k.at(zh=to // 2, zl=lax.rem(to, 2)), sems["z"] + d - 1)

    def end():
        me = 2 * k.zh + k.zl
        for d in range(1, 8):
            frm = lax.rem(me + 8 - d, 8)
            slot = buf.at[f32_z + frm]
            k.copy(slot, slot, k.at(zh=frm // 2, zl=lax.rem(frm, 2)), sems["z"] + d - 1).wait_recv()
        parts = [buf[f32_z + i] for i in range(8)]
        while len(parts) > 1:
            parts = [a + b for a, b in zip(parts[::2], parts[1::2])]
        out_ref[...] = parts[0]

    return [pair, x, y, z, end]


def sum_stages(k, grads, t_base, n_tiles, paired, first_in, second_in, z_in, gathered):
    halves = halves_of(n_tiles)
    piece_step, piece_size = pieces_of(n_tiles)
    sems = {}
    me = (k.x, k.y)

    def to_axis(half, step, delta):
        along = (half + step) % 2
        return k.at(x=mod4(k.x + delta)) if along == 0 else k.at(y=mod4(k.y + delta))

    def view(half, step, delta, part):
        t0, n = halves[half]
        along = (half + step) % 2
        dest = mod4(me[along] + delta)
        if step == 0:
            sub = pl.ds(0, 4) if part is None else pl.ds(2 * part, 2)
            return (
                paired.at[dest, sub, t0 : t0 + n]
                if along == 0
                else paired.at[sub, dest, t0 : t0 + n]
            )
        cut = (n + 1) // 2
        lo, hi = {None: (0, n), 0: (0, cut), 1: (cut, n)}[part]
        return (
            paired.at[dest, k.y, t0 + lo : t0 + hi]
            if along == 0
            else paired.at[k.x, dest, t0 + lo : t0 + hi]
        )

    def inbox(half, step, direction, part):
        n = halves[half][1]
        one = first_in[half] if step == 0 else second_in[half]
        box = one[2 + direction]
        if part is None:
            return box
        if step == 0:
            return box.at[2 * part : 2 * part + 2]
        cut = (n + 1) // 2
        return box.at[0:cut] if part == 0 else box.at[cut:n]

    def outset(half, step):
        one = first_in[half] if step == 0 else second_in[half]
        base = sems[half, step] = k.take(6)
        for direction, delta in ((0, 1), (1, -1)):
            k.start(
                view(half, step, 2, direction),
                one[direction],
                to_axis(half, step, delta),
                base + direction,
            )
        for direction, delta in ((0, 1), (1, -1)):
            part = 1 - direction
            k.start(
                view(half, step, delta, part),
                inbox(half, step, direction, part),
                to_axis(half, step, delta),
                base + 2 + direction,
            )

    def relay(half, step):
        one = first_in[half] if step == 0 else second_in[half]
        base = sems[half, step]
        for direction, delta in ((0, 1), (1, -1)):
            k.copy(
                one[direction], one[direction], to_axis(half, step, -delta), base + direction
            ).wait_recv()
            target = view(half, step, delta, direction)
            target[...] = target[...] + one[direction][...]
            k.start(
                target,
                inbox(half, step, direction, direction),
                to_axis(half, step, delta),
                base + 4 + direction,
            )

    def collect(half, step):
        base = sems[half, step]
        for direction, delta in ((0, 1), (1, -1)):
            for at, part in ((2, 1 - direction), (4, direction)):
                box = inbox(half, step, direction, part)
                k.copy(box, box, to_axis(half, step, -delta), base + at + direction).wait_recv()
        own = view(half, step, 0, None)
        f32 = jnp.float32
        own[...] = (
            own[...].astype(f32)
            + (inbox(half, step, 0, None)[...].astype(f32) + inbox(half, step, 1, None)[...].astype(f32))
        ).astype(jnp.bfloat16)

    def pair_out():
        sems["pair"] = k.take()
        k.start(grads.at[:, :, 1 - k.c, t_base : t_base + n_tiles], paired, k.at(c=1 - k.c), sems["pair"])

    def pair_in():
        k.copy(paired, paired, k.at(c=1 - k.c), sems["pair"]).wait_recv()

        @pl.loop(0, 4)
        def _(i):
            paired[i] = paired[i] + grads[i, :, k.c, t_base : t_base + n_tiles]

        for half in (0, 1):
            outset(half, 0)

    def relay_0():
        for half in (0, 1):
            relay(half, 0)

    def turn():
        for half in (0, 1):
            collect(half, 0)
            outset(half, 1)

    def relay_1():
        for half in (0, 1):
            relay(half, 1)

    def z_out():
        for half in (0, 1):
            collect(half, 1)
        base = sems["z"] = k.take(8)
        spot = 2 * k.zh + k.zl
        for q in range(4):
            for e in range(2):
                piece = piece_step * (2 * q + e)
                source = paired.at[k.x, k.y, piece : piece + piece_size]
                mine = (k.zh == q) & (k.c == e) & (k.zl == k.c)
                op = pltpu.make_async_remote_copy(
                    src_ref=source,
                    dst_ref=z_in.at[spot],
                    send_sem=k.send.at[base + 2 * q + e],
                    recv_sem=k.recv.at[base + spot],
                    device_id=k.at(zl=k.c, zh=q, c=e),
                    device_id_type=MESH,
                )

                @pl.when(jnp.logical_not(mine))
                def _():
                    op.start()

                @pl.when(mine)
                def _():
                    z_in[spot] = source[...]

                def done(op=op, mine=mine):
                    @pl.when(jnp.logical_not(mine))
                    def _():
                        op.wait_send()

                k.open.append(done)

    def z_in_sum():
        base = sems["z"]
        spot = 2 * k.zh + k.zl
        for slot in range(8):
            mine = (spot == slot) & (k.zl == k.c)

            @pl.when(jnp.logical_not(mine))
            def _():
                box = z_in.at[slot]
                k.copy(box, box, k.at(zh=slot // 2, zl=slot % 2, c=k.zl), base + slot).wait_recv()

        parts = [z_in[i].astype(jnp.float32) for i in range(8)]
        while len(parts) > 1:
            parts = [a + b for a, b in zip(parts[::2], parts[1::2])]
        p = 2 * k.zh + k.c
        gathered[p] = parts[0].astype(jnp.bfloat16)
        base = sems["g"] = k.take(7)
        for d in range(1, 8):
            to = lax.rem(p + d, 8)
            box = gathered.at[p]
            k.start(box, box, k.at(zh=to // 2, c=lax.rem(to, 2)), base + d - 1)

    def gather():
        p = 2 * k.zh + k.c
        for d in range(1, 8):
            frm = lax.rem(p + 8 - d, 8)
            box = gathered.at[frm]
            k.copy(box, box, k.at(zh=frm // 2, c=lax.rem(frm, 2)), sems["g"] + d - 1).wait_recv()

    return [pair_out, pair_in, relay_0, turn, relay_1, z_out, z_in_sum, gather]


def write_shard(t_base, n_tiles, gathered, grad_in_ref, grad_out_ref, scaling):
    piece_step, _ = pieces_of(n_tiles)
    for at in range(n_tiles):
        p = min(at // piece_step, 7)
        values = gathered[p, at - piece_step * p].astype(jnp.float32) * scaling
        tile = t_base + at
        if tile < 17:
            grad_in_ref[:, 128 * tile : 128 * tile + 128] = values
        else:
            column, half = (tile - 17) // 2, (tile - 17) % 2
            grad_out_ref[16 * half : 16 * half + 16, 128 * column : 128 * column + 128] = values


def sum_scratch(n_tiles):
    def tiles(*lead):
        return pltpu.VMEM((*lead, 16, 128), jnp.bfloat16)

    shapes = [tiles(4, 4, n_tiles)]
    for _, n in halves_of(n_tiles):
        shapes += [tiles(2, n)] * 2 + [tiles(4, n)] * 2
    for _, n in halves_of(n_tiles):
        cut = (n + 1) // 2
        shapes += [tiles(cut), tiles(n - cut), tiles(n), tiles(n)]
    return shapes + [tiles(8, pieces_of(n_tiles)[1])] * 2


def sum_refs(refs):
    return refs[0], (refs[1:5], refs[5:9]), (refs[9:13], refs[13:17]), refs[17], refs[18]


NN = (((1,), (0,)), ((), ()))
NT_DIMS = (((1,), (1,)), ((), ()))
TN = (((0,), (0,)), ((), ()))


def dot(a, b, dims=NN):
    return lax.dot_general(a, b, dims, preferred_element_type=F32)


def sigmoid(p):
    return 0.5 * jnp.tanh(0.5 * p) + 0.5


def cols(at, width=512):
    return slice(at, at + width)


def group_mask(unit):
    if unit == 0:
        return None
    row = lax.broadcasted_iota(jnp.int32, (BLOCK, BLOCK), 0)
    column = lax.broadcasted_iota(jnp.int32, (BLOCK, BLOCK), 1)
    return lax.rem(row, 16) == lax.rem(column, 16)


def positive_scores(unit, query, keyed):
    r = jnp.maximum(dot(query, keyed, NT_DIMS) * S ** (-0.5), 0.0)
    mask = group_mask(unit)
    return r if mask is None else jnp.where(mask, r, 0.0)


def length_of(unit):
    return BLOCK if unit == 0 else 16


def forward_group(m, unit, g, x):
    xf = x.astype(F32)
    scaling = lax.rsqrt(jnp.mean(xf * xf, axis=-1, keepdims=True) + EPSILON)
    hidden = (xf * scaling * m.gains[unit : unit + 1, :]).astype(BF16)
    m.hidden[unit, g] = hidden
    p = dot(hidden, m.w_in[unit, :, 2 * E :])
    m.proj[unit, g, :, 2 * E :] = p
    z = p * sigmoid(p)
    query = (z * m.scales[unit, 0:1, :]).astype(BF16)
    keyed = (z * m.scales[unit, 1:2, :]).astype(BF16)
    m.query[unit, g] = query
    m.keyed[unit, g] = keyed
    r = positive_scores(unit, query, keyed)
    weights = (r * r * (1.0 / length_of(unit))).astype(BF16)
    m.weights[unit, g] = weights
    for at in range(0, E, 512):
        p = dot(hidden, m.w_in[unit, :, cols(E + at)])
        m.proj[unit, g, :, cols(E + at)] = p
        m.value[unit, g, :, cols(at)] = (p * sigmoid(p)).astype(BF16)
        p = dot(hidden, m.w_in[unit, :, cols(at)])
        m.proj[unit, g, :, cols(at)] = p
        mixed = dot(weights, m.value[unit, g, :, cols(at)])
        m.mixed[unit, g, :, cols(at)] = mixed
        m.gated[unit, g, :, cols(at)] = (p * sigmoid(p) * mixed).astype(BF16)
    return (x.astype(F32) + dot(m.gated[unit, g], m.w_out[unit])).astype(BF16)


def backward_group(m, unit, g, x, upstream):
    for at in range(0, E, 512):
        d_gated = dot(upstream, m.w_out[unit, cols(at), :], NT_DIMS).astype(BF16).astype(F32)
        p = m.proj[unit, g, :, cols(at)]
        sig = sigmoid(p)
        gate = p * sig
        m.d_mixed[:, cols(at)] = (d_gated * gate).astype(BF16)
        slope = sig + gate * (1.0 - sig)
        m.d_proj[g, :, cols(at)] = (d_gated * m.mixed[unit, g, :, cols(at)] * slope).astype(BF16)
    d_weights = dot(m.d_mixed[...], m.value[unit, g], NT_DIMS).astype(BF16).astype(F32)
    query, keyed = m.query[unit, g], m.keyed[unit, g]
    r = positive_scores(unit, query, keyed)
    d_scores = (d_weights * r * (2.0 / length_of(unit) * S ** (-0.5))).astype(BF16)
    d_query = dot(d_scores, keyed).astype(BF16).astype(F32)
    d_keyed = dot(d_scores, query, TN).astype(BF16).astype(F32)
    p = m.proj[unit, g, :, 2 * E :]
    sig = sigmoid(p)
    z = p * sig
    d_z = d_query * m.scales[unit, 0:1, :] + d_keyed * m.scales[unit, 1:2, :]
    m.d_proj[g, :, 2 * E :] = (d_z * (sig + z * (1.0 - sig))).astype(BF16)
    m.small[unit, 4:5, :] += jnp.sum(d_query * z, axis=0, keepdims=True)
    m.small[unit, 5:6, :] += jnp.sum(d_keyed * z, axis=0, keepdims=True)
    weights = m.weights[unit, g]
    for at in range(0, E, 512):
        d_value = dot(weights, m.d_mixed[:, cols(at)], TN).astype(BF16).astype(F32)
        p = m.proj[unit, g, :, cols(E + at)]
        sig = sigmoid(p)
        m.d_proj[g, :, cols(E + at)] = (d_value * (sig + p * sig * (1.0 - sig))).astype(BF16)
    d_hidden = dot(m.d_proj[g], m.w_in[unit], NT_DIMS)
    xf = x.astype(F32)
    scaling = lax.rsqrt(jnp.mean(xf * xf, axis=-1, keepdims=True) + EPSILON)
    xs = xf * scaling
    d_gain = jnp.sum(d_hidden * xs, axis=0, keepdims=True)
    for i in range(4):
        m.small[unit, i : i + 1, :] += d_gain[:, 128 * i : 128 * i + 128]
    d_xs = d_hidden * m.gains[unit : unit + 1, :]
    d_x = scaling * (d_xs - xs * jnp.mean(d_xs * xs, axis=-1, keepdims=True))
    return (upstream.astype(F32) + d_x).astype(BF16)


def turned(m, unit):
    for g in (0, 1):
        m.hidden_t[unit, :, cols(BLOCK * g, BLOCK)] = m.hidden[unit, g].T
        m.gated_t[unit, :, cols(BLOCK * g, BLOCK)] = m.gated[unit, g].T


def weight_out_grad(m, unit, upstream):
    for i in range(4):
        rows = dot(m.gated_t[unit, cols(256 * i, 256), :], upstream).astype(BF16)
        parts = rows.reshape(4, 2, 2, 16, 512)
        for column in range(4):
            at = 17 + 2 * column
            m.grads[unit, i, :, :, at : at + 2] = parts[..., 128 * column : 128 * column + 128]


def weight_in_grad(m, unit):
    for at, width in ((0, 512), (512, 512), (1024, 512), (1536, 512), (2048, 128)):
        right = m.d_proj[:, :, cols(at, width)].reshape(2 * BLOCK, width)
        for i in (0, 1):
            part = dot(m.hidden_t[unit, cols(256 * i, 256), :], right).astype(BF16)
            part = part.reshape(2, 4, 2, 16, width)
            for j in range(width // 128):
                m.grads[unit, 2 * i : 2 * i + 2, :, :, at // 128 + j] = part[
                    ..., 128 * j : 128 * j + 128
                ]


class Memory:
    pass


SCRATCH = dict(
    w_in=((2, D, WIDE), BF16),
    w_out=((2, E, D), BF16),
    frames=((2, BLOCK, D), BF16),
    cot=((2, 8, 2, 16, D), BF16),
    first=((2, 8, 2, 16, D), BF16),
    first_pos=((2, 16, 16, D), BF16),
    cot_pos=((2, 16, 16, D), BF16),
    out_pos=((2, 16, 16, D), BF16),
    out=((2, 8, 2, 16, D), BF16),
    back_pos=((2, 16, 16, D), BF16),
    back=((2, 8, 2, 16, D), BF16),
    back_frames=((2, BLOCK, D), BF16),
    hidden=((2, 2, BLOCK, D), BF16),
    hidden_t=((2, D, 2 * BLOCK), BF16),
    proj=((2, 2, BLOCK, WIDE), F32),
    value=((2, 2, BLOCK, E), BF16),
    query=((2, 2, BLOCK, S), BF16),
    keyed=((2, 2, BLOCK, S), BF16),
    weights=((2, 2, BLOCK, BLOCK), BF16),
    mixed=((2, 2, BLOCK, E), F32),
    gated=((2, 2, BLOCK, E), BF16),
    gated_t=((2, E, 2 * BLOCK), BF16),
    d_mixed=((BLOCK, E), BF16),
    d_proj=((2, BLOCK, WIDE), BF16),
    grads=((2, 4, 4, 2, NT, 16, 128), BF16),
    small=((2, 8, 128), F32),
)
GROUPS = ((1, 0, NT), (0,) + OUT_TILES, (0,) + IN_TILES)


def step_kernel(scaling, *refs):
    m = Memory()
    frames_hbm, cot_hbm, w_in_hbm, w_out_hbm, m.scales, m.gains = refs[:6]
    out_hbm, back_hbm, in_ref, wout_ref, small_ref = refs[6:11]
    refs = refs[11:]
    for name, ref in zip(SCRATCH, refs):
        setattr(m, name, ref)
    refs = refs[len(SCRATCH) :]
    sums = []
    for unit, t0, n in GROUPS:
        sums.append(refs[:19])
        refs = refs[19:]
    small_bufs = refs[0]
    local, send, recv = refs[1:4]
    k = Links(send, recv)
    p = 2 * k.zh + k.c

    def load(src, dst, sem):
        op = pltpu.make_async_copy(src, dst, local.at[sem])
        op.start()
        return op

    loads = dict(
        frames=load(frames_hbm, m.frames, 0),
        in_0=load(w_in_hbm.at[0], m.w_in.at[0], 1),
        cot=load(cot_hbm, m.cot, 2),
        out_0=load(w_out_hbm.at[0], m.w_out.at[0], 3),
        in_1=load(w_in_hbm.at[1], m.w_in.at[1], 4),
        out_1=load(w_out_hbm.at[1], m.w_out.at[1], 5),
    )
    barrier(k)
    m.small[...] = jnp.zeros((2, 8, 128), F32)

    def peer(d):
        j = lax.rem(p + d, 8)
        return j, k.at(zh=j // 2, c=lax.rem(j, 2))

    def from_peer(d):
        j = lax.rem(p + 8 - d, 8)
        return j, k.at(zh=j // 2, c=lax.rem(j, 2))

    first_sems, cot_sems, out_sems, back_sems = k.take(28), k.take(14), k.take(14), k.take(28)

    def first_copy(b, h, d, to):
        sem = first_sems + (b * 2 + h) * 7 + d - 1
        return k.copy(m.first.at[b, to[0], h], m.first_pos.at[h, 2 * p + b], to[1], sem)

    def cot_copy(h, d, to):
        return k.copy(
            m.cot.at[:, to[0], h], m.cot_pos.at[h, pl.ds(2 * p, 2)], to[1], cot_sems + h * 7 + d - 1
        )

    def out_copy(h, d, to):
        return k.copy(
            m.out_pos.at[h, pl.ds(2 * to[0], 2)], m.out.at[:, p, h], to[1], out_sems + h * 7 + d - 1
        )

    def back_copy(b, h, d, to):
        sem = back_sems + (b * 2 + h) * 7 + d - 1
        return k.copy(m.back_pos.at[h, 2 * to[0] + b], m.back.at[b, p, h], to[1], sem)

    def send_cot(h):
        for d in range(1, 8):
            cot_copy(h, d, peer(d)).start()
        m.cot_pos[h, pl.ds(2 * p, 2)] = m.cot[:, p, h]

    def send_out(h):
        for d in range(1, 8):
            out_copy(h, d, peer(d)).start()

    loads["cot"].wait()
    send_cot(0)
    loads["frames"].wait()
    loads["in_0"].wait()
    loads["out_0"].wait()

    @pl.loop(0, 2)
    def _(b):
        m.first[b] = forward_group(m, 0, b, m.frames[b]).reshape(8, 2, 16, D)
        for h in (0, 1):
            for d in range(1, 8):
                first_copy(b, h, d, peer(d)).start()
        m.first_pos[:, 2 * p + b] = m.first[b, p]

    send_cot(1)
    turned(m, 0)
    loads["in_1"].wait()
    loads["out_1"].wait()

    @pl.loop(0, 2)
    def _(h):
        for b in (0, 1):
            for d in range(1, 8):
                first_copy(b, h, d, from_peer(d)).wait_recv()
        x = m.first_pos[h].reshape(BLOCK, D)
        m.out_pos[h] = forward_group(m, 1, h, x).reshape(16, 16, D)

        @pl.when(h == 0)
        def _():
            send_out(0)

        m.out[:, p, h] = m.out_pos[h, pl.ds(2 * p, 2)]

    @pl.loop(0, 2)
    def _(h):
        for d in range(1, 8):
            cot_copy(h, d, from_peer(d)).wait_recv()
        x = m.first_pos[h].reshape(BLOCK, D)
        upstream = m.cot_pos[h].reshape(BLOCK, D)
        m.back_pos[h] = backward_group(m, 1, h, x, upstream).reshape(16, 16, D)
        for b in (0, 1):
            for d in range(1, 8):
                back_copy(b, h, d, peer(d)).start()
        m.back[:, p, h] = m.back_pos[h, pl.ds(2 * p, 2)]

    send_out(1)
    turned(m, 1)

    late, early_out, early_in = (
        sum_stages(k, m.grads.at[unit], t0, n, *sum_refs(s)) for (unit, t0, n), s in zip(GROUPS, sums)
    )
    late_small = small_sum(k, small_bufs.at[1], m.small.at[1], small_ref.at[1])
    early_small = small_sum(k, small_bufs.at[0], m.small.at[0], small_ref.at[0])

    def run(*groups):
        for group in groups:
            if group:
                group.pop(0)()

    weight_out_grad(m, 1, m.cot_pos[...].reshape(2 * BLOCK, D))
    weight_in_grad(m, 1)
    run(late, late_small)
    run(late, late_small)

    def wait_back(b):
        for h in (0, 1):
            for d in range(1, 8):
                back_copy(b, h, d, from_peer(d)).wait_recv()

    wait_back(0)
    m.back_frames[0] = backward_group(m, 0, 0, m.frames[0], m.back[0].reshape(BLOCK, D))
    run(late, late_small)
    wait_back(1)
    weight_out_grad(m, 0, m.back[...].reshape(2 * BLOCK, D))
    run(early_out)
    run(late, late_small)
    m.back_frames[1] = backward_group(m, 0, 1, m.frames[1], m.back[1].reshape(BLOCK, D))
    store_back = load(m.back_frames, back_hbm, 0)
    run(early_out, early_small)
    run(late, late_small)
    weight_in_grad(m, 0)
    run(early_in)
    run(early_out, late, early_small)
    for h in (0, 1):
        for d in range(1, 8):
            out_copy(h, d, from_peer(d)).wait_recv()
    store_out = load(m.out, out_hbm, 2)
    while early_in:
        run(early_in, early_out, late, early_small)
    for (unit, t0, n), s in zip(GROUPS, sums):
        write_shard(t0, n, s[18], in_ref.at[unit], wout_ref.at[unit], scaling)
    small_ref[...] = small_ref[...] * scaling
    k.drain()

    @pl.loop(0, 2)
    def _(h):
        for d in range(1, 8):
            to = peer(d)
            cot_copy(h, d, to).wait_send()
            out_copy(h, d, to).wait_send()
            for b in (0, 1):
                first_copy(b, h, d, to).wait_send()
                back_copy(b, h, d, to).wait_send()

    store_back.wait()
    store_out.wait()


def on_device(frames, cotangent, weight_in, qk_scales, weight_out, gains):
    tokens_all = frames.shape[0] * frames.shape[1] * lax.axis_size(DP) * lax.axis_size(SEQ)
    vmem = pl.BlockSpec(memory_space=pltpu.VMEM)
    hbm = pl.BlockSpec(memory_space=pl.ANY)
    scratch = [pltpu.VMEM(shape, dtype) for shape, dtype in SCRATCH.values()]
    for _, _, n in GROUPS:
        scratch += sum_scratch(n)
    scratch += [pltpu.VMEM((2, 17, 8, 128), F32)]
    dma = pltpu.SemaphoreType.DMA
    scratch += [dma((6,)), dma((SEMS,)), dma((SEMS,))]
    result, back, grad_in, grad_out, small = pl.pallas_call(
        functools.partial(step_kernel, tokens_all ** (-0.5)),
        out_shape=(
            jax.ShapeDtypeStruct((2, 8, 2, 16, D), BF16),
            jax.ShapeDtypeStruct((2, BLOCK, D), BF16),
            jax.ShapeDtypeStruct((2, 16, WIDE), F32),
            jax.ShapeDtypeStruct((2, 32, D), F32),
            jax.ShapeDtypeStruct((2, 8, 128), F32),
        ),
        in_specs=[hbm, hbm, hbm, hbm, vmem, vmem],
        out_specs=(hbm, hbm, vmem, vmem, vmem),
        scratch_shapes=scratch,
        compiler_params=pltpu.CompilerParams(
            collective_id=0, has_side_effects=True, vmem_limit_bytes=67_043_328
        ),
    )(
        frames.reshape(2, BLOCK, D),
        cotangent.reshape(2, 8, 2, 16, D),
        weight_in,
        weight_out,
        qk_scales,
        gains,
    )
    return (
        result.reshape(frames.shape),
        back.reshape(frames.shape),
        grad_in,
        grad_out,
        small[:, :4].reshape(2, D),
        small[:, 4:6],
    )


def solution(mesh):
    split = Mesh(mesh.devices.reshape(4, 4, 2, 4, 2), DP + SEQ)
    placed = (P(DP, SEQ, None), P(DP, SEQ, None), P(), P(), P(), P())
    return jax.shard_map(
        on_device,
        mesh=split,
        in_specs=placed,
        out_specs=(
            P(DP, SEQ, None),
            P(DP, SEQ, None),
            P(None, DP, None),
            P(None, DP, None),
            P(),
            P(),
        ),
        check_vma=False,
    )
```

time: 199 us -> 118 us (0.59)
  Pallas kernels: 54.3 us -> 108 us
  matrix products: 42.5 us -> 0 us
  starting transfers between devices: 32.3 us -> 0 us
  local copies, waits for them, and re-layouts: 30.6 us -> 9.55 us
  other arithmetic: 18.5 us -> 0 us
  waiting for transfers between devices: 18.5 us -> 0 us
    pallas_call x1, Pallas kernels: 54.3 us -> 108 us  [on_device(): pl.pallas_call(functools.partial(step_kernel, tokens_all ** (-0.5)), out_...]
    dot_general x24 -> x0, matrix products: 42.5 us -> none  [the longest x2 12.1 us: unit_forward(): projected = jnp.dot(hidden, weight_in, preferred_element_type=jnp.float32)]
    all_to_all x4 -> x0, starting transfers between devices: 32.3 us -> none  [the longest x1 9.95 us: on_device(): lax.all_to_all(first, SEQ, split_axis=1, concat_axis=0, tiled=True)]
    all_to_all x4 -> x0, waiting for transfers between devices: 18.5 us -> none  [the longest x1 11.9 us: on_device(): lax.all_to_all(first, SEQ, split_axis=1, concat_axis=0, tiled=True)]
    reshape x9 -> x0, local copies, waits for them, and re-layouts: 17.5 us -> none  [the longest x4 11.1 us: as_tiles(): grad_in.astype(jnp.bfloat16).reshape(4, 4, 2, 16, 17, 128)]
    convert_element_type x8 -> x0, other arithmetic: 7.9 us -> none  [the longest x2 3.73 us: unit_backward(): grad_proj = grad_proj.astype(jnp.bfloat16)]
    another operation x4 -> x0, other arithmetic: 5.32 us -> none  [the longest x2 5.25 us: on_device(): jnp.stack([as_tiles(in_early, out_early), as_tiles(in_late, out_late)])]
    all_to_all x4 -> x0, local copies, waits for them, and re-layouts: 3.2 us -> none  [the longest x1 1.88 us: on_device(): lax.all_to_all(second, SEQ, split_axis=0, concat_axis=1, tiled=True)]
  transfers between devices with their start and end apart: 4 -> 0, of which waited for: 2 -> 0; matrix products, arithmetic and copies ran while one was open for 28% -> 0% of each run, Pallas kernels for 27% -> 0%
where the time goes in v2:
time: 118 us
  Pallas kernels  108 us (92%)
  local copies, waits for them, and re-layouts  9.55 us (8%)
    pallas_call x1, Pallas kernels, on_device(): pl.pallas_call(functools.partial(step_kernel, tokens_all ** (-0.5)), out_...  108 us
    unnamed x6, local copies, waits for them, and re-layouts  8.28 us

profile of v2, /device:TPU:1, one launch (start us, length us, event | category | flops | bytes accessed | tf_op | source)
XLA Modules:
  0.0 117.9 jit_solution(1692460536790390449)
XLA Ops:
  0.6 107.7 %shard_map.109 = (bf16[2,8,2,16,512]{4,3,2,1,0:T(8,128)(2,1)}, bf16[2,256,512]{2,1,0:T(8,128)(2,1)}, f32[2,16,2176]{2,1,0:T(8,128)}, f32[2,32,512]{2,1,0:T(8,128)}, f32[2,8,128]{2,1,0:T(8,128)}) custom-call(bf16[2,256,512]{2,1,0:T(8,128)(2,1)} %bitcast.11, bf16[2,8,2,16,512]{4,3,2,1,0:T(8,128)(2,1)} %bitcast.12, bf16[2,512,2176]{2,1,0:T(8,128)(2,1)} %refs_2_.1, ...), custom_call_target="tpu_custom_call" | custom-call | tf_op jit(solution)/shard_map/pallas_call | solution.py:713
  108.3 0.7 slice_bitcast_fusion
  109.0 0.6 copy.14
  109.6 1.3 %slice.7 = f32[2,2,128]{2,1,0:T(2,128)} slice(f32[2,8,128]{2,1,0:T(8,128)} %get-tuple-element.15), slice={[0:2], [4:6], [0:128]} | slice | bytes 4096 | tf_op jit(solution)/shard_map/slice | solution.py:742
  110.9 1.9 %copy.19 = bf16[1,512,512]{2,1,0:T(8,128)(2,1)} copy(bf16[1,512,512]{2,1,0:T(8,128)(2,1)} %bitcast.10) | data formatting | bytes 1048576
  112.8 1.9 %copy.20 = bf16[1,512,512]{2,1,0:T(8,128)(2,1)} copy(bf16[1,512,512]{2,1,0:T(8,128)(2,1)} %bitcast.9) | data formatting | bytes 1048576
  114.6 1.7 %copy.21 = f32[2,16,2176]{2,1,0:T(8,128)} copy(f32[2,16,2176]{2,1,0:T(8,128)} %get-tuple-element.24) | data formatting | bytes 557056
  116.3 1.6 %copy.22 = f32[2,32,512]{2,1,0:T(8,128)} copy(f32[2,32,512]{2,1,0:T(8,128)} %get-tuple-element.25) | data formatting | bytes 262144

commit v3 on v2

--- a/solution.py
+++ b/solution.py
@@ -15,7 +15,6 @@
 EPSILON = 1e-06
 F32, BF16 = jnp.float32, jnp.bfloat16
 NT = 25
-IN_TILES, OUT_TILES = (0, 17), (17, 8)
 SEMS = 300
 
 
@@ -79,7 +78,7 @@
     return lax.rem(v + 4, 4)
 
 
-def barrier(k):
+def greet(k):
     sem = pltpu.get_barrier_semaphore()
     targets = [k.at(x=mod4(k.x + d)) for d in (1, 2, 3)]
     targets += [k.at(y=mod4(k.y + d)) for d in (1, 2, 3)]
@@ -92,7 +91,7 @@
                     )
     for target in targets:
         pl.semaphore_signal(sem, inc=1, device_id=target, device_id_type=MESH)
-    pl.semaphore_wait(sem, len(targets))
+    return lambda: pl.semaphore_wait(sem, len(targets))
 
 
 def small_sum(k, buf, value_ref, out_ref):
@@ -147,7 +146,7 @@
     return [pair, x, y, z, end]
 
 
-def sum_stages(k, grads, t_base, n_tiles, paired, first_in, second_in, z_in, gathered):
+def sum_stages(k, grads, t_base, n_tiles, direct, paired, first_in, second_in, z_in, gathered):
     halves = halves_of(n_tiles)
     piece_step, piece_size = pieces_of(n_tiles)
     sems = {}
@@ -325,23 +324,94 @@
             box = gathered.at[frm]
             k.copy(box, box, k.at(zh=frm // 2, c=lax.rem(frm, 2)), sems["g"] + d - 1).wait_recv()
 
+    spot = 2 * k.zh + k.zl
+    holds = k.zl == k.c
+
+    def whole_copy(q):
+        return pltpu.make_async_remote_copy(
+            src_ref=paired.at[k.x, k.y],
+            dst_ref=z_in.at[spot],
+            send_sem=k.send.at[sems["z"] + q],
+            recv_sem=k.recv.at[sems["z"] + spot],
+            device_id=k.at(zl=k.c, zh=q),
+            device_id_type=MESH,
+        )
+
+    def whole_out():
+        for half in (0, 1):
+            collect(half, 1)
+        sems["z"] = k.take(8)
+        for q in range(4):
+            mine = holds & (k.zh == q)
+            op = whole_copy(q)
+
+            @pl.when(jnp.logical_not(mine))
+            def _():
+                op.start()
+
+            def done(op=op, mine=mine):
+                @pl.when(jnp.logical_not(mine))
+                def _():
+                    op.wait_send()
+
+            k.open.append(done)
+
+        @pl.when(holds)
+        def _():
+            z_in[spot] = paired[k.x, k.y]
+
+    def whole_sum():
+        sems["g"] = k.take()
+        across = k.copy(gathered, gathered, k.at(c=1 - k.c), sems["g"])
+
+        @pl.when(holds)
+        def _():
+            for slot in range(8):
+
+                @pl.when(spot != slot)
+                def _():
+                    box = z_in.at[slot]
+                    k.copy(
+                        box, box, k.at(zh=slot // 2, zl=slot % 2), sems["z"] + slot
+                    ).wait_recv()
+
+            parts = [z_in[i].astype(jnp.float32) for i in range(8)]
+            while len(parts) > 1:
+                parts = [a + b for a, b in zip(parts[::2], parts[1::2])]
+            gathered[0] = parts[0].astype(jnp.bfloat16)
+            across.start()
+
+        def done():
+            @pl.when(holds)
+            def _():
+                across.wait_send()
+
+        k.open.append(done)
+
+    def whole_in():
+        @pl.when(jnp.logical_not(holds))
+        def _():
+            k.copy(gathered, gathered, k.at(c=1 - k.c), sems["g"]).wait_recv()
+
+    if direct:
+        return [pair_out, pair_in, relay_0, turn, relay_1, whole_out, whole_sum, whole_in]
     return [pair_out, pair_in, relay_0, turn, relay_1, z_out, z_in_sum, gather]
 
 
-def write_shard(t_base, n_tiles, gathered, grad_in_ref, grad_out_ref, scaling):
-    piece_step, _ = pieces_of(n_tiles)
+def write_shard(t_base, n_tiles, direct, gathered, grad_in_ref, grad_out_ref, scaling):
+    piece_step = n_tiles if direct else pieces_of(n_tiles)[0]
     for at in range(n_tiles):
         p = min(at // piece_step, 7)
         values = gathered[p, at - piece_step * p].astype(jnp.float32) * scaling
         tile = t_base + at
-        if tile < 17:
-            grad_in_ref[:, 128 * tile : 128 * tile + 128] = values
+        if tile < 8:
+            column, half = tile // 2, tile % 2
+            grad_out_ref[16 * half : 16 * half + 16, 128 * column : 128 * column + 128] = values
         else:
-            column, half = (tile - 17) // 2, (tile - 17) % 2
-            grad_out_ref[16 * half : 16 * half + 16, 128 * column : 128 * column + 128] = values
-
-
-def sum_scratch(n_tiles):
+            grad_in_ref[:, 128 * (tile - 8) : 128 * (tile - 7)] = values
+
+
+def sum_scratch(n_tiles, direct):
     def tiles(*lead):
         return pltpu.VMEM((*lead, 16, 128), jnp.bfloat16)
 
@@ -351,6 +421,8 @@
     for _, n in halves_of(n_tiles):
         cut = (n + 1) // 2
         shapes += [tiles(cut), tiles(n - cut), tiles(n), tiles(n)]
+    if direct:
+        return shapes + [tiles(8, n_tiles), tiles(1, n_tiles)]
     return shapes + [tiles(8, pieces_of(n_tiles)[1])] * 2
 
 
@@ -420,16 +492,19 @@
     return (x.astype(F32) + dot(m.gated[unit, g], m.w_out[unit])).astype(BF16)
 
 
-def backward_group(m, unit, g, x, upstream):
+def backward_gate(m, unit, g, upstream):
     for at in range(0, E, 512):
         d_gated = dot(upstream, m.w_out[unit, cols(at), :], NT_DIMS).astype(BF16).astype(F32)
         p = m.proj[unit, g, :, cols(at)]
         sig = sigmoid(p)
         gate = p * sig
-        m.d_mixed[:, cols(at)] = (d_gated * gate).astype(BF16)
+        m.d_mixed[g, :, cols(at)] = (d_gated * gate).astype(BF16)
         slope = sig + gate * (1.0 - sig)
         m.d_proj[g, :, cols(at)] = (d_gated * m.mixed[unit, g, :, cols(at)] * slope).astype(BF16)
-    d_weights = dot(m.d_mixed[...], m.value[unit, g], NT_DIMS).astype(BF16).astype(F32)
+
+
+def backward_attention(m, unit, g):
+    d_weights = dot(m.d_mixed[g], m.value[unit, g], NT_DIMS).astype(BF16).astype(F32)
     query, keyed = m.query[unit, g], m.keyed[unit, g]
     r = positive_scores(unit, query, keyed)
     d_scores = (d_weights * r * (2.0 / length_of(unit) * S ** (-0.5))).astype(BF16)
@@ -444,10 +519,13 @@
     m.small[unit, 5:6, :] += jnp.sum(d_keyed * z, axis=0, keepdims=True)
     weights = m.weights[unit, g]
     for at in range(0, E, 512):
-        d_value = dot(weights, m.d_mixed[:, cols(at)], TN).astype(BF16).astype(F32)
+        d_value = dot(weights, m.d_mixed[g, :, cols(at)], TN).astype(BF16).astype(F32)
         p = m.proj[unit, g, :, cols(E + at)]
         sig = sigmoid(p)
         m.d_proj[g, :, cols(E + at)] = (d_value * (sig + p * sig * (1.0 - sig))).astype(BF16)
+
+
+def backward_input(m, unit, g, x, upstream):
     d_hidden = dot(m.d_proj[g], m.w_in[unit], NT_DIMS)
     xf = x.astype(F32)
     scaling = lax.rsqrt(jnp.mean(xf * xf, axis=-1, keepdims=True) + EPSILON)
@@ -471,18 +549,22 @@
         rows = dot(m.gated_t[unit, cols(256 * i, 256), :], upstream).astype(BF16)
         parts = rows.reshape(4, 2, 2, 16, 512)
         for column in range(4):
-            at = 17 + 2 * column
+            at = 2 * column
             m.grads[unit, i, :, :, at : at + 2] = parts[..., 128 * column : 128 * column + 128]
 
 
-def weight_in_grad(m, unit):
-    for at, width in ((0, 512), (512, 512), (1024, 512), (1536, 512), (2048, 128)):
+GATE = ((0, 512), (512, 512))
+OTHERS = ((1024, 512), (1536, 512), (2048, 128))
+
+
+def weight_in_grad(m, unit, columns):
+    for at, width in columns:
         right = m.d_proj[:, :, cols(at, width)].reshape(2 * BLOCK, width)
         for i in (0, 1):
             part = dot(m.hidden_t[unit, cols(256 * i, 256), :], right).astype(BF16)
             part = part.reshape(2, 4, 2, 16, width)
             for j in range(width // 128):
-                m.grads[unit, 2 * i : 2 * i + 2, :, :, at // 128 + j] = part[
+                m.grads[unit, 2 * i : 2 * i + 2, :, :, 8 + at // 128 + j] = part[
                     ..., 128 * j : 128 * j + 128
                 ]
 
@@ -514,12 +596,12 @@
     mixed=((2, 2, BLOCK, E), F32),
     gated=((2, 2, BLOCK, E), BF16),
     gated_t=((2, E, 2 * BLOCK), BF16),
-    d_mixed=((BLOCK, E), BF16),
+    d_mixed=((2, BLOCK, E), BF16),
     d_proj=((2, BLOCK, WIDE), BF16),
     grads=((2, 4, 4, 2, NT, 16, 128), BF16),
     small=((2, 8, 128), F32),
 )
-GROUPS = ((1, 0, NT), (0,) + OUT_TILES, (0,) + IN_TILES)
+GROUPS = ((1, 0, NT, False), (0, 0, 16, False), (0, 16, 9, True))
 
 
 def step_kernel(scaling, *refs):
@@ -531,7 +613,7 @@
         setattr(m, name, ref)
     refs = refs[len(SCRATCH) :]
     sums = []
-    for unit, t0, n in GROUPS:
+    for _ in GROUPS:
         sums.append(refs[:19])
         refs = refs[19:]
     small_bufs = refs[0]
@@ -544,15 +626,15 @@
         op.start()
         return op
 
+    met = greet(k)
     loads = dict(
         frames=load(frames_hbm, m.frames, 0),
         in_0=load(w_in_hbm.at[0], m.w_in.at[0], 1),
+        out_0=load(w_out_hbm.at[0], m.w_out.at[0], 3),
         cot=load(cot_hbm, m.cot, 2),
-        out_0=load(w_out_hbm.at[0], m.w_out.at[0], 3),
         in_1=load(w_in_hbm.at[1], m.w_in.at[1], 4),
         out_1=load(w_out_hbm.at[1], m.w_out.at[1], 5),
     )
-    barrier(k)
     m.small[...] = jnp.zeros((2, 8, 128), F32)
 
     def peer(d):
@@ -563,141 +645,158 @@
         j = lax.rem(p + 8 - d, 8)
         return j, k.at(zh=j // 2, c=lax.rem(j, 2))
 
-    first_sems, cot_sems, out_sems, back_sems = k.take(28), k.take(14), k.take(14), k.take(28)
-
-    def first_copy(b, h, d, to):
-        sem = first_sems + (b * 2 + h) * 7 + d - 1
-        return k.copy(m.first.at[b, to[0], h], m.first_pos.at[h, 2 * p + b], to[1], sem)
+    first_sems, cot_sems, out_sems, back_sems = (k.take(14) for _ in range(4))
+
+    def first_copy(h, d, to):
+        box = m.first_pos.at[h, pl.ds(2 * p, 2)]
+        return k.copy(m.first.at[:, to[0], h], box, to[1], first_sems + h * 7 + d - 1)
 
     def cot_copy(h, d, to):
-        return k.copy(
-            m.cot.at[:, to[0], h], m.cot_pos.at[h, pl.ds(2 * p, 2)], to[1], cot_sems + h * 7 + d - 1
-        )
+        box = m.cot_pos.at[h, pl.ds(2 * p, 2)]
+        return k.copy(m.cot.at[:, to[0], h], box, to[1], cot_sems + h * 7 + d - 1)
 
     def out_copy(h, d, to):
-        return k.copy(
-            m.out_pos.at[h, pl.ds(2 * to[0], 2)], m.out.at[:, p, h], to[1], out_sems + h * 7 + d - 1
-        )
-
-    def back_copy(b, h, d, to):
-        sem = back_sems + (b * 2 + h) * 7 + d - 1
-        return k.copy(m.back_pos.at[h, 2 * to[0] + b], m.back.at[b, p, h], to[1], sem)
-
-    def send_cot(h):
+        box = m.out.at[:, p, h]
+        return k.copy(m.out_pos.at[h, pl.ds(2 * to[0], 2)], box, to[1], out_sems + h * 7 + d - 1)
+
+    def back_copy(h, d, to):
+        box = m.back.at[:, p, h]
+        return k.copy(m.back_pos.at[h, pl.ds(2 * to[0], 2)], box, to[1], back_sems + h * 7 + d - 1)
+
+    def send(copy, h):
         for d in range(1, 8):
-            cot_copy(h, d, peer(d)).start()
-        m.cot_pos[h, pl.ds(2 * p, 2)] = m.cot[:, p, h]
-
-    def send_out(h):
+            copy(h, d, peer(d)).start()
+
+    def receive(copy, h):
         for d in range(1, 8):
-            out_copy(h, d, peer(d)).start()
-
-    loads["cot"].wait()
-    send_cot(0)
+            copy(h, d, from_peer(d)).wait_recv()
+
     loads["frames"].wait()
     loads["in_0"].wait()
     loads["out_0"].wait()
-
-    @pl.loop(0, 2)
-    def _(b):
-        m.first[b] = forward_group(m, 0, b, m.frames[b]).reshape(8, 2, 16, D)
-        for h in (0, 1):
-            for d in range(1, 8):
-                first_copy(b, h, d, peer(d)).start()
-        m.first_pos[:, 2 * p + b] = m.first[b, p]
-
-    send_cot(1)
-    turned(m, 0)
+    with jax.named_scope("f0"):
+
+        @pl.loop(0, 2)
+        def _(b):
+            m.first[b] = forward_group(m, 0, b, m.frames[b]).reshape(8, 2, 16, D)
+
+    with jax.named_scope("barrier"):
+        met()
+    for h in (0, 1):
+        send(first_copy, h)
+        m.first_pos[h, pl.ds(2 * p, 2)] = m.first[:, p, h]
+    loads["cot"].wait()
+    for h in (0, 1):
+        send(cot_copy, h)
+        m.cot_pos[h, pl.ds(2 * p, 2)] = m.cot[:, p, h]
+    with jax.named_scope("turn0"):
+        turned(m, 0)
     loads["in_1"].wait()
     loads["out_1"].wait()
 
     @pl.loop(0, 2)
     def _(h):
-        for b in (0, 1):
-            for d in range(1, 8):
-                first_copy(b, h, d, from_peer(d)).wait_recv()
-        x = m.first_pos[h].reshape(BLOCK, D)
-        m.out_pos[h] = forward_group(m, 1, h, x).reshape(16, 16, D)
-
-        @pl.when(h == 0)
-        def _():
-            send_out(0)
-
-        m.out[:, p, h] = m.out_pos[h, pl.ds(2 * p, 2)]
+        with jax.named_scope("w_first"):
+            receive(first_copy, h)
+        with jax.named_scope("f1"):
+            x = m.first_pos[h].reshape(BLOCK, D)
+            m.out_pos[h] = forward_group(m, 1, h, x).reshape(16, 16, D)
+
+    m.out[:, p] = m.out_pos[:, pl.ds(2 * p, 2)].transpose(1, 0, 2, 3)
+    with jax.named_scope("turn1"):
+        turned(m, 1)
 
     @pl.loop(0, 2)
     def _(h):
-        for d in range(1, 8):
-            cot_copy(h, d, from_peer(d)).wait_recv()
-        x = m.first_pos[h].reshape(BLOCK, D)
-        upstream = m.cot_pos[h].reshape(BLOCK, D)
-        m.back_pos[h] = backward_group(m, 1, h, x, upstream).reshape(16, 16, D)
-        for b in (0, 1):
-            for d in range(1, 8):
-                back_copy(b, h, d, peer(d)).start()
+        with jax.named_scope("w_cot"):
+            receive(cot_copy, h)
+        with jax.named_scope("b1"):
+            x = m.first_pos[h].reshape(BLOCK, D)
+            upstream = m.cot_pos[h].reshape(BLOCK, D)
+            backward_gate(m, 1, h, upstream)
+            backward_attention(m, 1, h)
+            m.back_pos[h] = backward_input(m, 1, h, x, upstream).reshape(16, 16, D)
+        send(back_copy, h)
         m.back[:, p, h] = m.back_pos[h, pl.ds(2 * p, 2)]
 
-    send_out(1)
-    turned(m, 1)
-
-    late, early_out, early_in = (
-        sum_stages(k, m.grads.at[unit], t0, n, *sum_refs(s)) for (unit, t0, n), s in zip(GROUPS, sums)
+    late, early, last = (
+        sum_stages(k, m.grads.at[unit], t0, n, direct, *sum_refs(s))
+        for (unit, t0, n, direct), s in zip(GROUPS, sums)
     )
     late_small = small_sum(k, small_bufs.at[1], m.small.at[1], small_ref.at[1])
     early_small = small_sum(k, small_bufs.at[0], m.small.at[0], small_ref.at[0])
+    names = dict(zip(map(id, (late, early, last)), ("late", "early", "last")))
 
     def run(*groups):
         for group in groups:
             if group:
-                group.pop(0)()
-
-    weight_out_grad(m, 1, m.cot_pos[...].reshape(2 * BLOCK, D))
-    weight_in_grad(m, 1)
+                with jax.named_scope(f"{names.get(id(group), 'small')}{8 - len(group)}"):
+                    group.pop(0)()
+
+    with jax.named_scope("wg1"):
+        weight_out_grad(m, 1, m.cot_pos[...].reshape(2 * BLOCK, D))
+        weight_in_grad(m, 1, GATE + OTHERS)
     run(late, late_small)
     run(late, late_small)
-
-    def wait_back(b):
-        for h in (0, 1):
+    with jax.named_scope("w_back"):
+        receive(back_copy, 0)
+        receive(back_copy, 1)
+    for h in (0, 1):
+        send(out_copy, h)
+    with jax.named_scope("gate0"):
+        for g in (0, 1):
+            backward_gate(m, 0, g, m.back[g].reshape(BLOCK, D))
+    with jax.named_scope("wg0"):
+        weight_out_grad(m, 0, m.back[...].reshape(2 * BLOCK, D))
+        weight_in_grad(m, 0, GATE)
+    run(early, late)
+    with jax.named_scope("attn0"):
+        for g in (0, 1):
+            backward_attention(m, 0, g)
+    run(early)
+    with jax.named_scope("wg0b"):
+        weight_in_grad(m, 0, OTHERS)
+    run(last, late, late_small)
+    with jax.named_scope("input0"):
+        for g in (0, 1):
+            m.back_frames[g] = backward_input(m, 0, g, m.frames[g], m.back[g].reshape(BLOCK, D))
+    store_back = load(m.back_frames, back_hbm, 0)
+    run(early_small, last, early, late, late_small)
+    run(last, early_small, early, late, late_small)
+    run(last, early_small, early, late, late_small)
+    with jax.named_scope("w_out"):
+        receive(out_copy, 0)
+        receive(out_copy, 1)
+    store_out = load(m.out, out_hbm, 2)
+    while last or early or late or early_small or late_small:
+        run(last, early_small, early, late, late_small)
+    with jax.named_scope("write"):
+        for (unit, t0, n, direct), s in zip(GROUPS, sums):
+            write_shard(t0, n, direct, s[18], in_ref.at[unit], wout_ref.at[unit], scaling)
+        small_ref[...] = small_ref[...] * scaling
+    with jax.named_scope("drain"):
+        k.drain()
+
+        @pl.loop(0, 2)
+        def _(h):
             for d in range(1, 8):
-                back_copy(b, h, d, from_peer(d)).wait_recv()
-
-    wait_back(0)
-    m.back_frames[0] = backward_group(m, 0, 0, m.frames[0], m.back[0].reshape(BLOCK, D))
-    run(late, late_small)
-    wait_back(1)
-    weight_out_grad(m, 0, m.back[...].reshape(2 * BLOCK, D))
-    run(early_out)
-    run(late, late_small)
-    m.back_frames[1] = backward_group(m, 0, 1, m.frames[1], m.back[1].reshape(BLOCK, D))
-    store_back = load(m.back_frames, back_hbm, 0)
-    run(early_out, early_small)
-    run(late, late_small)
-    weight_in_grad(m, 0)
-    run(early_in)
-    run(early_out, late, early_small)
-    for h in (0, 1):
-        for d in range(1, 8):
-            out_copy(h, d, from_peer(d)).wait_recv()
-    store_out = load(m.out, out_hbm, 2)
-    while early_in:
-        run(early_in, early_out, late, early_small)
-    for (unit, t0, n), s in zip(GROUPS, sums):
-        write_shard(t0, n, s[18], in_ref.at[unit], wout_ref.at[unit], scaling)
-    small_ref[...] = small_ref[...] * scaling
-    k.drain()
-
-    @pl.loop(0, 2)
-    def _(h):
-        for d in range(1, 8):
-            to = peer(d)
-            cot_copy(h, d, to).wait_send()
-            out_copy(h, d, to).wait_send()
-            for b in (0, 1):
-                first_copy(b, h, d, to).wait_send()
-                back_copy(b, h, d, to).wait_send()
-
-    store_back.wait()
-    store_out.wait()
+                to = peer(d)
+                for copy in (first_copy, cot_copy, out_copy, back_copy):
+                    copy(h, d, to).wait_send()
+
+        store_back.wait()
+        store_out.wait()
+
+
+def write_kernel(result, back, grad_in, grad_out, small, o_result, o_back, o_in, o_out, o_gains, o_scales):
+    o_result[...] = result[...].reshape(o_result.shape)
+    o_back[...] = back[...].reshape(o_back.shape)
+    o_in[...] = grad_in[...]
+    o_out[...] = grad_out[...]
+    for unit in (0, 1):
+        for i in range(4):
+            o_gains[unit : unit + 1, 128 * i : 128 * i + 128] = small[unit, i : i + 1, :]
+        o_scales[unit] = small[unit, 4:6, :]
 
 
 def on_device(frames, cotangent, weight_in, qk_scales, weight_out, gains):
@@ -705,12 +804,12 @@
     vmem = pl.BlockSpec(memory_space=pltpu.VMEM)
     hbm = pl.BlockSpec(memory_space=pl.ANY)
     scratch = [pltpu.VMEM(shape, dtype) for shape, dtype in SCRATCH.values()]
-    for _, _, n in GROUPS:
-        scratch += sum_scratch(n)
+    for _, _, n, direct in GROUPS:
+        scratch += sum_scratch(n, direct)
     scratch += [pltpu.VMEM((2, 17, 8, 128), F32)]
     dma = pltpu.SemaphoreType.DMA
     scratch += [dma((6,)), dma((SEMS,)), dma((SEMS,))]
-    result, back, grad_in, grad_out, small = pl.pallas_call(
+    parts = pl.pallas_call(
         functools.partial(step_kernel, tokens_all ** (-0.5)),
         out_shape=(
             jax.ShapeDtypeStruct((2, 8, 2, 16, D), BF16),
@@ -733,14 +832,19 @@
         qk_scales,
         gains,
     )
-    return (
-        result.reshape(frames.shape),
-        back.reshape(frames.shape),
-        grad_in,
-        grad_out,
-        small[:, :4].reshape(2, D),
-        small[:, 4:6],
-    )
+    return pl.pallas_call(
+        write_kernel,
+        out_shape=(
+            jax.ShapeDtypeStruct(frames.shape, BF16),
+            jax.ShapeDtypeStruct(frames.shape, BF16),
+            jax.ShapeDtypeStruct((2, 16, WIDE), F32),
+            jax.ShapeDtypeStruct((2, 32, D), F32),
+            jax.ShapeDtypeStruct((2, D), F32),
+            jax.ShapeDtypeStruct((2, 2, S), F32),
+        ),
+        in_specs=[vmem] * 5,
+        out_specs=(vmem,) * 6,
+    )(*parts)
 
 
 def solution(mesh):

time: 118 us -> 95.4 us (0.81)
  Pallas kernels: 108 us -> 94.6 us
  local copies, waits for them, and re-layouts: 9.55 us -> 0 us
    pallas_call x1, Pallas kernels: 108 us -> 92.1 us  [on_device(): pl.pallas_call(functools.partial(step_kernel, tokens_all ** (-0.5)), out_...]
    unnamed x6 -> x0, local copies, waits for them, and re-layouts: 8.28 us -> none
    pallas_call x0 -> x1, Pallas kernels: none -> 2.45 us  [on_device(): pl.pallas_call(write_kernel, out_shape=(jax.ShapeDtypeStruct(frames.shape...]
    slice x1 -> x0, local copies, waits for them, and re-layouts: 1.28 us -> none  [on_device(): small[:, 4:6]]
where the time goes in v3:
time: 95.4 us; the launch traced here: 95.2 us
  Pallas kernels  94.6 us (99%)
    pallas_call x1, Pallas kernels, on_device(): pl.pallas_call(functools.partial(step_kernel, tokens_all ** (-0.5)), out_...  92.1 us
    pallas_call x1, Pallas kernels, on_device(): pl.pallas_call(write_kernel, out_shape=(jax.ShapeDtypeStruct(frames.shape...  2.45 us

profile of v3, /device:TPU:1, one launch (start us, length us, event | category | flops | bytes accessed | tf_op | source)
XLA Modules:
  0.0 95.2 jit_solution(16473691505291188992)
XLA Ops:
  0.6 92.1 %shard_map.109 = (bf16[2,8,2,16,512]{4,3,2,1,0:T(8,128)(2,1)}, bf16[2,256,512]{2,1,0:T(8,128)(2,1)}, f32[2,16,2176]{2,1,0:T(8,128)}, f32[2,32,512]{2,1,0:T(8,128)}, f32[2,8,128]{2,1,0:T(8,128)}) custom-call(bf16[2,256,512]{2,1,0:T(8,128)(2,1)} %bitcast.2, bf16[2,8,2,16,512]{4,3,2,1,0:T(8,128)(2,1)} %bitcast.3, bf16[2,512,2176]{2,1,0:T(8,128)(2,1)} %refs_2_.1, ...), custom_call_target="tpu_custom_call" | custom-call | tf_op jit(solution)/shard_map/pallas_call | solution.py:812
  92.8 2.5 %shard_map.110 = (bf16[1,512,512]{2,1,0:T(8,128)(2,1)}, bf16[1,512,512]{2,1,0:T(8,128)(2,1)}, f32[2,16,2176]{2,1,0:T(8,128)}, f32[2,32,512]{2,1,0:T(8,128)}, f32[2,512]{1,0:T(2,128)}, /*index=5*/f32[2,2,128]{2,1,0:T(2,128)}) custom-call(bf16[2,8,2,16,512]{4,3,2,1,0:T(8,128)(2,1)} %get-tuple-element.11.result, bf16[2,256,512]{2,1,0:T(8,128)(2,1)} %get-tuple-element.12.back, ...), custom_call_target="tpu_custom_call" | custom-call | tf_op jit(solution)/shard_map/pallas_call | solution.py:835

commit v4 on v3

v4 whole, which is shorter than its diff:
```python
import functools

import jax
import jax.numpy as jnp
from jax import lax
from jax.experimental import pallas as pl
from jax.experimental.pallas import tpu as pltpu
from jax.sharding import Mesh
from jax.sharding import PartitionSpec as P

DP = ("dp_0", "dp_1", "dp_2")
SEQ = ("seq_0", "seq_1")
D, E, S, BLOCK = 512, 1024, 128, 256
WIDE = 2 * E + S
EPSILON = 1e-06
F32, BF16 = jnp.float32, jnp.bfloat16
NT = 25
SEMS = 60


MESH = pl.DeviceIdType.MESH


def halves_of(n):
    return ((0, (n + 1) // 2), ((n + 1) // 2, n // 2))


def pieces_of(n):
    return n // 8, n - 7 * (n // 8)


class Links:
    def __init__(self, send, recv):
        self.send, self.recv, self.used, self.waits = send, recv, 0, []
        self.x, self.y, self.zl = (lax.axis_index(a) for a in DP)
        self.zh, self.c = (lax.axis_index(a) for a in SEQ)

    def take(self, count=1):
        at = self.used
        self.used += count
        return at

    def at(self, x=None, y=None, zl=None, zh=None, c=None):
        return (
            self.x if x is None else x,
            self.y if y is None else y,
            self.zl if zl is None else zl,
            self.zh if zh is None else zh,
            self.c if c is None else c,
        )

    def copy(self, src, dst, target, sem):
        return pltpu.make_async_remote_copy(
            src_ref=src,
            dst_ref=dst,
            send_sem=self.send.at[sem],
            recv_sem=self.recv.at[sem],
            device_id=target,
            device_id_type=MESH,
        )

    def whole(self, region, sem):
        return self.copy(region, region, self.at(c=1 - self.c), sem)

    def arrived(self, region, sem):
        self.whole(region, sem).wait_recv()

    def later(self, region, sem, when=None):
        def wait():
            if when is None:
                self.whole(region, sem).wait_send()
            else:

                @pl.when(when)
                def _():
                    self.whole(region, sem).wait_send()

        self.waits.append(wait)

    def drain(self):
        for wait in self.waits:
            wait()


def mod4(v):
    return lax.rem(v + 8, 4)


def greet(k):
    sem = pltpu.get_barrier_semaphore()
    targets = [k.at(x=mod4(k.x + d)) for d in (1, 2, 3)]
    targets += [k.at(y=mod4(k.y + d)) for d in (1, 2, 3)]
    for dl in (0, 1):
        for dh in range(4):
            for dc in (0, 1):
                if dl or dh or dc:
                    targets.append(
                        k.at(zl=lax.rem(k.zl + dl, 2), zh=mod4(k.zh + dh), c=lax.rem(k.c + dc, 2))
                    )
    for target in targets:
        pl.semaphore_signal(sem, inc=1, device_id=target, device_id_type=MESH)
    return lambda: pl.semaphore_wait(sem, len(targets))


def tree_sum(parts):
    while len(parts) > 1:
        parts = [a + b for a, b in zip(parts[::2], parts[1::2])]
    return parts[0]


def small_sum(k, buf, value_ref, out_ref):
    sems = {}
    axes = (
        ("z", 8, 1, 2 * k.zh + k.zl, lambda i: k.at(zh=i // 2, zl=lax.rem(i, 2))),
        ("x", 4, 9, k.x, lambda i: k.at(x=i)),
        ("y", 4, 13, k.y, lambda i: k.at(y=i)),
    )

    def share(axis, value):
        name, size, first, me, target = axis
        buf[first + me] = value
        sem = sems[name] = k.take()
        box = buf.at[first + me]
        for d in range(1, size):
            k.copy(box, box, target(lax.rem(me + d, size)), sem).start()
        k.later(buf.at[first : first + size - 1], sem)

    def collected(axis):
        name, size, first, _, _ = axis
        k.arrived(buf.at[first : first + size - 1], sems[name])
        return tree_sum([buf[first + i] for i in range(size)])

    def pair():
        sems["p"] = k.take()
        k.copy(value_ref, buf.at[0], k.at(c=1 - k.c), sems["p"]).start()
        k.later(buf.at[0], sems["p"])

    def z():
        k.arrived(buf.at[0], sems["p"])
        share(axes[0], value_ref[...] + buf[0])

    def x():
        share(axes[1], collected(axes[0]))

    def y():
        share(axes[2], collected(axes[1]))

    def end():
        out_ref[...] = collected(axes[2])

    return [pair, z, x, y, end]


def sum_stages(k, grads, cuts, direct, paired, first_in, second_in, z_in, gathered):
    sems = {}
    me = (k.x, k.y)
    t_base, n_tiles = cuts[0], cuts[-1] - cuts[0]
    halves = halves_of(n_tiles)
    f32 = jnp.float32

    def to_axis(half, step, delta):
        along = (half + step) % 2
        return k.at(x=mod4(k.x + delta)) if along == 0 else k.at(y=mod4(k.y + delta))

    def view(half, step, delta, part=None):
        t0, n = halves[half]
        along = (half + step) % 2
        dest = mod4(me[along] + delta)
        if step == 0:
            sub = pl.ds(0, 4) if part is None else pl.ds(2 * part, 2)
            at = (dest, sub) if along == 0 else (sub, dest)
        else:
            at = (dest, k.y) if along == 0 else (k.x, dest)
        return paired.at[at[0], at[1], t0 : t0 + n]

    def pair_copy(i):
        lo, hi = cuts[i], cuts[i + 1]
        return k.copy(
            grads.at[:, :, 1 - k.c, lo:hi],
            paired.at[:, :, lo - t_base : hi - t_base],
            k.at(c=1 - k.c),
            sems["pair", i],
        )

    def pair_out(i):
        sems["pair", i] = k.take()
        op = pair_copy(i)
        op.start()
        k.waits.append(op.wait_send)

    def pair_in():
        for i in range(len(cuts) - 1):
            pair_copy(i).wait_recv()

        @pl.loop(0, 4)
        def _(i):
            paired[i] = paired[i] + grads[i, :, k.c, t_base : t_base + n_tiles]

        for half in (0, 1):
            spread(half, 0) if direct else outset(half)

    def spread(half, step):
        box = (first_in if step == 0 else second_in)[half]
        sem = sems[half, step] = k.take()
        for d in (2, 1, 3):
            k.copy(view(half, step, d), box.at[d - 1], to_axis(half, step, d), sem).start()
        k.later(box, sem)

    def collect_spread(half, step):
        box = (first_in if step == 0 else second_in)[half]
        k.arrived(box, sems[half, step])
        own = view(half, step, 0)
        near = box[0].astype(f32) + box[2].astype(f32)
        own[...] = ((own[...].astype(f32) + box[1].astype(f32)) + near).astype(jnp.bfloat16)

    def outset(half):
        one, two = first_in[half][:2], first_in[half][2:]
        base = sems[half, 0] = k.take(4)
        for direction, delta in ((0, 1), (1, -1)):
            k.copy(
                view(half, 0, 2, direction), one[direction], to_axis(half, 0, delta), base + direction
            ).start()
            k.later(one[direction], base + direction)
        for direction, delta in ((0, 1), (1, -1)):
            part = 1 - direction
            k.copy(
                view(half, 0, delta, part),
                two[direction].at[2 * part : 2 * part + 2],
                to_axis(half, 0, delta),
                base + 2 + direction,
            ).start()

    def relay():
        for half in (0, 1):
            one, two = first_in[half][:2], first_in[half][2:]
            base = sems[half, 0]
            for direction, delta in ((0, 1), (1, -1)):
                k.arrived(one[direction], base + direction)
                target = view(half, 0, delta, direction)
                target[...] = target[...] + one[direction][...]
                k.copy(
                    target,
                    two[direction].at[2 * direction : 2 * direction + 2],
                    to_axis(half, 0, delta),
                    base + 2 + direction,
                ).start()
                k.later(two[direction], base + 2 + direction)

    def collect(half):
        two = first_in[half][2:]
        for direction in (0, 1):
            k.arrived(two[direction], sems[half, 0] + 2 + direction)
        own = view(half, 0, 0)
        own[...] = (
            own[...].astype(f32) + (two[0][...].astype(f32) + two[1][...].astype(f32))
        ).astype(jnp.bfloat16)

    def turn():
        for half in (0, 1):
            collect_spread(half, 0) if direct else collect(half)
            spread(half, 1)

    spot = 2 * k.zh + k.zl
    holds = k.zl == k.c
    piece_step, piece_size = pieces_of(n_tiles)

    def z_out():
        for half in (0, 1):
            collect_spread(half, 1)
        sem = sems["z"] = k.take()
        for q in range(4):
            for e in range(2):
                piece = piece_step * (2 * q + e)
                source = paired.at[k.x, k.y, piece : piece + piece_size]
                mine = (k.zh == q) & (k.c == e) & holds
                op = k.copy(source, z_in.at[spot], k.at(zl=k.c, zh=q, c=e), sem)

                @pl.when(jnp.logical_not(mine))
                def _():
                    op.start()

                @pl.when(mine)
                def _():
                    z_in[spot] = source[...]

        k.later(z_in.at[0:7], sem, holds)
        k.later(z_in, sem, jnp.logical_not(holds))

    def z_sum():
        @pl.when(holds)
        def _():
            k.arrived(z_in.at[0:7], sems["z"])

        @pl.when(jnp.logical_not(holds))
        def _():
            k.arrived(z_in, sems["z"])

        p = 2 * k.zh + k.c
        gathered[p] = tree_sum([z_in[i].astype(f32) for i in range(8)]).astype(jnp.bfloat16)
        sem = sems["g"] = k.take()
        box = gathered.at[p]
        for d in range(1, 8):
            to = lax.rem(p + d, 8)
            k.copy(box, box, k.at(zh=to // 2, c=lax.rem(to, 2)), sem).start()
        k.later(gathered.at[0:7], sem)

    def gather():
        k.arrived(gathered.at[0:7], sems["g"])

    def whole_out():
        for half in (0, 1):
            collect_spread(half, 1)
        sem = sems["z"] = k.take()
        for q in range(4):
            op = k.copy(paired.at[k.x, k.y], z_in.at[spot], k.at(zl=k.c, zh=q), sem)

            @pl.when(jnp.logical_not(holds & (k.zh == q)))
            def _():
                op.start()

        @pl.when(holds)
        def _():
            z_in[spot] = paired[k.x, k.y]

        k.later(z_in.at[0:3], sem, holds)
        k.later(z_in.at[0:4], sem, jnp.logical_not(holds))

    def whole_sum():
        sems["g"] = k.take()

        @pl.when(holds)
        def _():
            k.arrived(z_in.at[0:7], sems["z"])
            gathered[0] = tree_sum([z_in[i].astype(f32) for i in range(8)]).astype(jnp.bfloat16)
            k.whole(gathered, sems["g"]).start()

        k.later(gathered, sems["g"], holds)

    def whole_in():
        @pl.when(jnp.logical_not(holds))
        def _():
            k.arrived(gathered, sems["g"])

    pairs = [functools.partial(pair_out, i) for i in range(len(cuts) - 1)]
    if direct:
        return pairs + [pair_in, turn, whole_out, whole_sum, whole_in]
    return pairs + [pair_in, relay, turn, z_out, z_sum, gather]


def write_shard(cuts, direct, gathered, grad_in_ref, grad_out_ref, scaling):
    t_base, n_tiles = cuts[0], cuts[-1] - cuts[0]
    piece_step = n_tiles if direct else pieces_of(n_tiles)[0]
    for at in range(n_tiles):
        p = min(at // piece_step, 7)
        values = gathered[p, at - piece_step * p].astype(jnp.float32) * scaling
        tile = t_base + at
        if tile < 8:
            column, half = tile // 2, tile % 2
            grad_out_ref[16 * half : 16 * half + 16, 128 * column : 128 * column + 128] = values
        else:
            grad_in_ref[:, 128 * (tile - 8) : 128 * (tile - 7)] = values


def sum_scratch(cuts, direct):
    n_tiles = cuts[-1] - cuts[0]

    def tiles(*lead):
        return pltpu.VMEM((*lead, 16, 128), jnp.bfloat16)

    shapes = [tiles(4, 4, n_tiles)]
    if direct:
        for lead in ((3, 4), (3,)):
            shapes += [tiles(*lead, n) for _, n in halves_of(n_tiles)]
        return shapes + [tiles(8, n_tiles), tiles(1, n_tiles)]
    for _, n in halves_of(n_tiles):
        shapes += [tiles(2, n)] * 2 + [tiles(4, n)] * 2
    shapes += [tiles(3, n) for _, n in halves_of(n_tiles)]
    return shapes + [tiles(8, pieces_of(n_tiles)[1])] * 2


def sum_refs(refs, direct):
    if direct:
        return refs[0], refs[1:3], refs[3:5], refs[5], refs[6]
    return refs[0], (refs[1:5], refs[5:9]), refs[9:11], refs[11], refs[12]


NN = (((1,), (0,)), ((), ()))
NT_DIMS = (((1,), (1,)), ((), ()))
TN = (((0,), (0,)), ((), ()))


def dot(a, b, dims=NN):
    return lax.dot_general(a, b, dims, preferred_element_type=F32)


def sigmoid(p):
    return 0.5 * jnp.tanh(0.5 * p) + 0.5


def cols(at, width=512):
    return slice(at, at + width)


def group_mask(unit):
    if unit == 0:
        return None
    row = lax.broadcasted_iota(jnp.int32, (BLOCK, BLOCK), 0)
    column = lax.broadcasted_iota(jnp.int32, (BLOCK, BLOCK), 1)
    return lax.rem(row, 16) == lax.rem(column, 16)


def positive_scores(unit, query, keyed):
    r = jnp.maximum(dot(query, keyed, NT_DIMS) * S ** (-0.5), 0.0)
    mask = group_mask(unit)
    return r if mask is None else jnp.where(mask, r, 0.0)


def length_of(unit):
    return BLOCK if unit == 0 else 16


def forward_group(m, unit, g, x):
    xf = x.astype(F32)
    scaling = lax.rsqrt(jnp.mean(xf * xf, axis=-1, keepdims=True) + EPSILON)
    hidden = (xf * scaling * m.gains[unit : unit + 1, :]).astype(BF16)
    m.hidden[unit, g] = hidden
    p = dot(hidden, m.w_in[unit, :, 2 * E :])
    m.proj[unit, g, :, 2 * E :] = p
    z = p * sigmoid(p)
    query = (z * m.scales[unit, 0:1, :]).astype(BF16)
    keyed = (z * m.scales[unit, 1:2, :]).astype(BF16)
    m.query[unit, g] = query
    m.keyed[unit, g] = keyed
    r = positive_scores(unit, query, keyed)
    weights = (r * r * (1.0 / length_of(unit))).astype(BF16)
    m.weights[unit, g] = weights
    for at in range(0, E, 512):
        p = dot(hidden, m.w_in[unit, :, cols(E + at)])
        m.proj[unit, g, :, cols(E + at)] = p
        m.value[unit, g, :, cols(at)] = (p * sigmoid(p)).astype(BF16)
        p = dot(hidden, m.w_in[unit, :, cols(at)])
        m.proj[unit, g, :, cols(at)] = p
        mixed = dot(weights, m.value[unit, g, :, cols(at)])
        m.mixed[unit, g, :, cols(at)] = mixed
        m.gated[unit, g, :, cols(at)] = (p * sigmoid(p) * mixed).astype(BF16)
    return (x.astype(F32) + dot(m.gated[unit, g], m.w_out[unit])).astype(BF16)


def backward_gate(m, unit, g, upstream):
    for at in range(0, E, 512):
        d_gated = dot(upstream, m.w_out[unit, cols(at), :], NT_DIMS).astype(BF16).astype(F32)
        p = m.proj[unit, g, :, cols(at)]
        sig = sigmoid(p)
        gate = p * sig
        m.d_mixed[g, :, cols(at)] = (d_gated * gate).astype(BF16)
        slope = sig + gate * (1.0 - sig)
        m.d_proj[g, :, cols(at)] = (d_gated * m.mixed[unit, g, :, cols(at)] * slope).astype(BF16)


def backward_attention(m, unit, g):
    d_weights = dot(m.d_mixed[g], m.value[unit, g], NT_DIMS).astype(BF16).astype(F32)
    query, keyed = m.query[unit, g], m.keyed[unit, g]
    r = positive_scores(unit, query, keyed)
    d_scores = (d_weights * r * (2.0 / length_of(unit) * S ** (-0.5))).astype(BF16)
    d_query = dot(d_scores, keyed).astype(BF16).astype(F32)
    d_keyed = dot(d_scores, query, TN).astype(BF16).astype(F32)
    p = m.proj[unit, g, :, 2 * E :]
    sig = sigmoid(p)
    z = p * sig
    d_z = d_query * m.scales[unit, 0:1, :] + d_keyed * m.scales[unit, 1:2, :]
    m.d_proj[g, :, 2 * E :] = (d_z * (sig + z * (1.0 - sig))).astype(BF16)
    m.small[unit, 4:5, :] += jnp.sum(d_query * z, axis=0, keepdims=True)
    m.small[unit, 5:6, :] += jnp.sum(d_keyed * z, axis=0, keepdims=True)
    weights = m.weights[unit, g]
    for at in range(0, E, 512):
        d_value = dot(weights, m.d_mixed[g, :, cols(at)], TN).astype(BF16).astype(F32)
        p = m.proj[unit, g, :, cols(E + at)]
        sig = sigmoid(p)
        m.d_proj[g, :, cols(E + at)] = (d_value * (sig + p * sig * (1.0 - sig))).astype(BF16)


def backward_input(m, unit, g, x, upstream):
    d_hidden = dot(m.d_proj[g], m.w_in[unit], NT_DIMS)
    xf = x.astype(F32)
    scaling = lax.rsqrt(jnp.mean(xf * xf, axis=-1, keepdims=True) + EPSILON)
    xs = xf * scaling
    d_gain = jnp.sum(d_hidden * xs, axis=0, keepdims=True)
    for i in range(4):
        m.small[unit, i : i + 1, :] += d_gain[:, 128 * i : 128 * i + 128]
    d_xs = d_hidden * m.gains[unit : unit + 1, :]
    d_x = scaling * (d_xs - xs * jnp.mean(d_xs * xs, axis=-1, keepdims=True))
    return (upstream.astype(F32) + d_x).astype(BF16)


def turned(m, unit):
    for g in (0, 1):
        m.hidden_t[unit, :, cols(BLOCK * g, BLOCK)] = m.hidden[unit, g].T
        m.gated_t[unit, :, cols(BLOCK * g, BLOCK)] = m.gated[unit, g].T


def weight_out_grad(m, unit, upstream):
    for i in range(4):
        rows = dot(m.gated_t[unit, cols(256 * i, 256), :], upstream).astype(BF16)
        parts = rows.reshape(4, 2, 2, 16, 512)
        for column in range(4):
            at = 2 * column
            m.grads[unit, i, :, :, at : at + 2] = parts[..., 128 * column : 128 * column + 128]


GATE = ((0, 512), (512, 512))
OTHERS = ((1024, 512), (1536, 512), (2048, 128))


def weight_in_grad(m, unit, columns):
    for at, width in columns:
        right = m.d_proj[:, :, cols(at, width)].reshape(2 * BLOCK, width)
        for i in (0, 1):
            part = dot(m.hidden_t[unit, cols(256 * i, 256), :], right).astype(BF16)
            part = part.reshape(2, 4, 2, 16, width)
            for j in range(width // 128):
                m.grads[unit, 2 * i : 2 * i + 2, :, :, 8 + at // 128 + j] = part[
                    ..., 128 * j : 128 * j + 128
                ]


class Memory:
    pass


SCRATCH = dict(
    w_in=((2, D, WIDE), BF16),
    w_out=((2, E, D), BF16),
    frames=((2, BLOCK, D), BF16),
    cot=((2, 8, 2, 16, D), BF16),
    first=((2, 8, 2, 16, D), BF16),
    first_pos=((2, 16, 16, D), BF16),
    cot_pos=((2, 16, 16, D), BF16),
    out_pos=((2, 16, 16, D), BF16),
    out=((2, 8, 2, 16, D), BF16),
    back_pos=((2, 16, 16, D), BF16),
    back=((2, 8, 2, 16, D), BF16),
    back_frames=((2, BLOCK, D), BF16),
    hidden=((2, 2, BLOCK, D), BF16),
    hidden_t=((2, D, 2 * BLOCK), BF16),
    proj=((2, 2, BLOCK, WIDE), F32),
    value=((2, 2, BLOCK, E), BF16),
    query=((2, 2, BLOCK, S), BF16),
    keyed=((2, 2, BLOCK, S), BF16),
    weights=((2, 2, BLOCK, BLOCK), BF16),
    mixed=((2, 2, BLOCK, E), F32),
    gated=((2, 2, BLOCK, E), BF16),
    gated_t=((2, E, 2 * BLOCK), BF16),
    d_mixed=((2, BLOCK, E), BF16),
    d_proj=((2, BLOCK, WIDE), BF16),
    grads=((2, 4, 4, 2, NT, 16, 128), BF16),
    small=((2, 8, 128), F32),
    scales=((2, 2, S), F32),
    gains=((2, D), F32),
)
GROUPS = (
    (1, (0, 8, 16), False),
    (1, (16, 25), False),
    (0, (0, 8, 16), False),
    (0, (16, 25), True),
)


def step_kernel(scaling, *refs):
    m = Memory()
    frames_hbm, cot_hbm, w_in_hbm, w_out_hbm, scales_hbm, gains_hbm = refs[:6]
    out_hbm, back_hbm, in_ref, wout_ref, small_ref = refs[6:11]
    refs = refs[11:]
    for name, ref in zip(SCRATCH, refs):
        setattr(m, name, ref)
    refs = refs[len(SCRATCH) :]
    sums = []
    for _, cuts, direct in GROUPS:
        count = len(sum_scratch(cuts, direct))
        sums.append(sum_refs(refs[:count], direct))
        refs = refs[count:]
    small_bufs = refs[0]
    local, send, recv = refs[1:4]
    k = Links(send, recv)
    p = 2 * k.zh + k.c

    def load(src, dst, sem):
        op = pltpu.make_async_copy(src, dst, local.at[sem])
        op.start()
        return op

    loads = dict(
        frames=load(frames_hbm, m.frames, 0),
        scales=load(scales_hbm, m.scales, 6),
        gains=load(gains_hbm, m.gains, 7),
        others_0=load(w_in_hbm.at[0, :, E:], m.w_in.at[0, :, E:], 1),
        gate_0=load(w_in_hbm.at[0, :, :E], m.w_in.at[0, :, :E], 8),
        out_0=load(w_out_hbm.at[0], m.w_out.at[0], 3),
    )
    met = greet(k)
    m.small[...] = jnp.zeros((2, 8, 128), F32)

    def peer(d):
        j = lax.rem(p + d, 8)
        return j, k.at(zh=j // 2, c=lax.rem(j, 2))

    def from_peer(d):
        j = lax.rem(p + 8 - d, 8)
        return j, k.at(zh=j // 2, c=lax.rem(j, 2))

    first_sems, cot_sems, out_sems, back_sems = (k.take(2) for _ in range(4))

    def first_copy(b, h, d, to):
        return k.copy(m.first.at[b, to[0], h], m.first_pos.at[h, 2 * p + b], to[1], first_sems + h)

    def cot_copy(h, d, to):
        box = m.cot_pos.at[h, pl.ds(2 * p, 2)]
        return k.copy(m.cot.at[:, to[0], h], box, to[1], cot_sems + h)

    def out_copy(h, d, to):
        box = m.out.at[:, p, h]
        return k.copy(m.out_pos.at[h, pl.ds(2 * to[0], 2)], box, to[1], out_sems + h)

    def back_copy(h, d, to):
        box = m.back.at[:, p, h]
        return k.copy(m.back_pos.at[h, pl.ds(2 * to[0], 2)], box, to[1], back_sems + h)

    def send(copy, h):
        for d in range(1, 8):
            copy(h, d, peer(d)).start()

    def receive(base, h):
        k.arrived(m.first_pos.at[0, 0:14], base + h)

    for name in ("frames", "scales", "gains", "others_0", "gate_0", "out_0"):
        loads[name].wait()
    loads = dict(
        cot=load(cot_hbm, m.cot, 2),
        in_1=load(w_in_hbm.at[1], m.w_in.at[1], 4),
        out_1=load(w_out_hbm.at[1], m.w_out.at[1], 5),
    )

    def exchange_first(b, h):
        for d in range(1, 8):
            first_copy(b, h, d, peer(d)).start()

    def block_forward(b):
        with jax.named_scope("f0"):
            m.first[b] = forward_group(m, 0, b, m.frames[b]).reshape(8, 2, 16, D)

    block_forward(0)
    with jax.named_scope("barrier"):
        met()
    for h in (0, 1):
        exchange_first(0, h)
    block_forward(1)
    for h in (0, 1):
        exchange_first(1, h)
        m.first_pos[h, pl.ds(2 * p, 2)] = m.first[:, p, h]
    loads["cot"].wait()
    for h in (0, 1):
        send(cot_copy, h)
        m.cot_pos[h, pl.ds(2 * p, 2)] = m.cot[:, p, h]
    with jax.named_scope("turn0"):
        turned(m, 0)
    loads["in_1"].wait()
    loads["out_1"].wait()

    @pl.loop(0, 2)
    def _(h):
        with jax.named_scope("w_first"):
            receive(first_sems, h)
        with jax.named_scope("f1"):
            x = m.first_pos[h].reshape(BLOCK, D)
            m.out_pos[h] = forward_group(m, 1, h, x).reshape(16, 16, D)

    m.out[:, p] = m.out_pos[:, pl.ds(2 * p, 2)].transpose(1, 0, 2, 3)
    with jax.named_scope("turn1"):
        turned(m, 1)

    groups = {}
    for name, (unit, cuts, direct), refs_of in zip(("a1", "b1", "a0", "b0"), GROUPS, sums):
        groups[name] = sum_stages(k, m.grads.at[unit], cuts, direct, *refs_of)
    groups["s"] = small_sum(k, small_bufs, m.small, small_ref)
    done = dict.fromkeys(groups, 0)

    def run(names):
        for name in names.split():
            with jax.named_scope(f"{name}_{done[name]}"):
                groups[name][done[name]]()
            done[name] += 1

    def unit_1_gate(h, wait=True):
        if wait:
            with jax.named_scope("w_cot"):
                receive(cot_sems, h)
        with jax.named_scope("gate1"):
            backward_gate(m, 1, h, m.cot_pos[h].reshape(BLOCK, D))

    def unit_1_rest(h):
        with jax.named_scope("rest1"):
            backward_attention(m, 1, h)
            x = m.first_pos[h].reshape(BLOCK, D)
            upstream = m.cot_pos[h].reshape(BLOCK, D)
            m.back_pos[h] = backward_input(m, 1, h, x, upstream).reshape(16, 16, D)
        send(back_copy, h)
        m.back[:, p, h] = m.back_pos[h, pl.ds(2 * p, 2)]

    def input_0(g):
        with jax.named_scope("input0"):
            m.back_frames[g] = backward_input(m, 0, g, m.frames[g], m.back[g].reshape(BLOCK, D))

    def write(at):
        unit, cuts, direct = GROUPS[at]
        write_shard(cuts, direct, sums[at][-1], in_ref.at[unit], wout_ref.at[unit], scaling)

    unit_1_gate(0)
    unit_1_rest(0)
    with jax.named_scope("w_cot"):
        receive(cot_sems, 1)
    with jax.named_scope("wgo1"):
        weight_out_grad(m, 1, m.cot_pos[...].reshape(2 * BLOCK, D))
    run("a1")
    unit_1_gate(1, False)
    with jax.named_scope("wgi1"):
        weight_in_grad(m, 1, GATE)
    run("a1")
    unit_1_rest(1)
    run("a1")
    with jax.named_scope("wg1b"):
        weight_in_grad(m, 1, OTHERS)
    run("b1 b1 a1")
    with jax.named_scope("w_back"):
        receive(back_sems, 0)
        receive(back_sems, 1)
    for h in (0, 1):
        send(out_copy, h)
    with jax.named_scope("wgo0"):
        weight_out_grad(m, 0, m.back[...].reshape(2 * BLOCK, D))
    run("a0")
    with jax.named_scope("gate0"):
        for g in (0, 1):
            backward_gate(m, 0, g, m.back[g].reshape(BLOCK, D))
    run("b1")
    with jax.named_scope("wgi0"):
        weight_in_grad(m, 0, GATE)
    run("a0 a1")
    with jax.named_scope("attn0"):
        for g in (0, 1):
            backward_attention(m, 0, g)
    run("b1 a0")
    with jax.named_scope("wg0b"):
        weight_in_grad(m, 0, OTHERS)
    run("b0")
    input_0(0)
    run("a1")
    input_0(1)
    store_back = load(m.back_frames, back_hbm, 0)
    run("s b0 a0 s b1 b0 a0 s a1 b1 b0 a0 s")
    with jax.named_scope("w_out"):
        receive(out_sems, 0)
        receive(out_sems, 1)
    store_out = load(m.out, out_hbm, 2)
    run("a0 s a1 b1")
    write(0)
    write(1)
    small_ref[...] = small_ref[...] * scaling
    run("b0 a0")
    write(2)
    run("b0")
    write(3)
    with jax.named_scope("drain"):
        k.drain()

        for base in (first_sems, cot_sems, out_sems, back_sems):
            for h in (0, 1):
                k.whole(m.first_pos.at[0, 0:14], base + h).wait_send()

        store_back.wait()
        store_out.wait()
    assert all(done[name] == len(stages) for name, stages in groups.items())
    assert k.used <= SEMS


def write_kernel(result, back, grad_in, grad_out, small, o_result, o_back, o_in, o_out, o_gains, o_scales):
    o_result[...] = result[...].reshape(o_result.shape)
    o_back[...] = back[...].reshape(o_back.shape)
    o_in[...] = grad_in[...]
    o_out[...] = grad_out[...]
    for unit in (0, 1):
        for i in range(4):
            o_gains[unit : unit + 1, 128 * i : 128 * i + 128] = small[unit, i : i + 1, :]
        o_scales[unit] = small[unit, 4:6, :]


def on_device(frames, cotangent, weight_in, qk_scales, weight_out, gains):
    tokens_all = frames.shape[0] * frames.shape[1] * lax.axis_size(DP) * lax.axis_size(SEQ)
    vmem = pl.BlockSpec(memory_space=pltpu.VMEM)
    hbm = pl.BlockSpec(memory_space=pl.ANY)
    scratch = [pltpu.VMEM(shape, dtype) for shape, dtype in SCRATCH.values()]
    for _, cuts, direct in GROUPS:
        scratch += sum_scratch(cuts, direct)
    scratch += [pltpu.VMEM((17, 2, 8, 128), F32)]
    dma = pltpu.SemaphoreType.DMA
    scratch += [dma((9,)), dma((SEMS,)), dma((SEMS,))]
    parts = pl.pallas_call(
        functools.partial(step_kernel, tokens_all ** (-0.5)),
        out_shape=(
            jax.ShapeDtypeStruct((2, 8, 2, 16, D), BF16),
            jax.ShapeDtypeStruct((2, BLOCK, D), BF16),
            jax.ShapeDtypeStruct((2, 16, WIDE), F32),
            jax.ShapeDtypeStruct((2, 32, D), F32),
            jax.ShapeDtypeStruct((2, 8, 128), F32),
        ),
        in_specs=[hbm] * 6,
        out_specs=(hbm, hbm, vmem, vmem, vmem),
        scratch_shapes=scratch,
        compiler_params=pltpu.CompilerParams(
            collective_id=0, has_side_effects=True, vmem_limit_bytes=67_043_328
        ),
    )(
        frames.reshape(2, BLOCK, D),
        cotangent.reshape(2, 8, 2, 16, D),
        weight_in,
        weight_out,
        qk_scales,
        gains,
    )
    return pl.pallas_call(
        write_kernel,
        out_shape=(
            jax.ShapeDtypeStruct(frames.shape, BF16),
            jax.ShapeDtypeStruct(frames.shape, BF16),
            jax.ShapeDtypeStruct((2, 16, WIDE), F32),
            jax.ShapeDtypeStruct((2, 32, D), F32),
            jax.ShapeDtypeStruct((2, D), F32),
            jax.ShapeDtypeStruct((2, 2, S), F32),
        ),
        in_specs=[vmem] * 5,
        out_specs=(vmem,) * 6,
    )(*parts)


def solution(mesh):
    split = Mesh(mesh.devices.reshape(4, 4, 2, 4, 2), DP + SEQ)
    placed = (P(DP, SEQ, None), P(DP, SEQ, None), P(), P(), P(), P())
    return jax.shard_map(
        on_device,
        mesh=split,
        in_specs=placed,
        out_specs=(
            P(DP, SEQ, None),
            P(DP, SEQ, None),
            P(None, DP, None),
            P(None, DP, None),
            P(),
            P(),
        ),
        check_vma=False,
    )
```

time: 95.4 us -> 86.5 us (0.907)
  Pallas kernels: 94.6 us -> 85.7 us
    pallas_call x1, Pallas kernels: 92.1 us -> 83.3 us  [on_device(): pl.pallas_call(functools.partial(step_kernel, tokens_all ** (-0.5)), out_...]
where the time goes in v4:
time: 86.5 us; the launch traced here: 86.4 us
  Pallas kernels  85.7 us (99%)
    pallas_call x1, Pallas kernels, on_device(): pl.pallas_call(functools.partial(step_kernel, tokens_all ** (-0.5)), out_...  83.3 us
    pallas_call x1, Pallas kernels, on_device(): pl.pallas_call(write_kernel, out_shape=(jax.ShapeDtypeStruct(frames.shape...  2.45 us

profile of v4, /device:TPU:1, one launch (start us, length us, event | category | flops | bytes accessed | tf_op | source)
XLA Modules:
  0.0 86.4 jit_solution(7738873424786105768)
XLA Ops:
  0.6 83.3 %shard_map.109 = (bf16[2,8,2,16,512]{4,3,2,1,0:T(8,128)(2,1)}, bf16[2,256,512]{2,1,0:T(8,128)(2,1)}, f32[2,16,2176]{2,1,0:T(8,128)}, f32[2,32,512]{2,1,0:T(8,128)}, f32[2,8,128]{2,1,0:T(8,128)}) custom-call(bf16[2,256,512]{2,1,0:T(8,128)(2,1)} %bitcast.2, bf16[2,8,2,16,512]{4,3,2,1,0:T(8,128)(2,1)} %bitcast.3, bf16[2,512,2176]{2,1,0:T(8,128)(2,1)} %refs_2_.1, ...), custom_call_target="tpu_custom_call" | custom-call | tf_op jit(solution)/shard_map/pallas_call | solution.py:805
  83.9 2.5 %shard_map.110 = (bf16[1,512,512]{2,1,0:T(8,128)(2,1)}, bf16[1,512,512]{2,1,0:T(8,128)(2,1)}, f32[2,16,2176]{2,1,0:T(8,128)}, f32[2,32,512]{2,1,0:T(8,128)}, f32[2,512]{1,0:T(2,128)}, /*index=5*/f32[2,2,128]{2,1,0:T(2,128)}) custom-call(bf16[2,8,2,16,512]{4,3,2,1,0:T(8,128)(2,1)} %get-tuple-element.11.result, bf16[2,256,512]{2,1,0:T(8,128)(2,1)} %get-tuple-element.12.back, ...), custom_call_target="tpu_custom_call" | custom-call | tf_op jit(solution)/shard_map/pallas_call | solution.py:828

commit v5 on v4

--- a/solution.py
+++ b/solution.py
@@ -15,7 +15,7 @@
 EPSILON = 1e-06
 F32, BF16 = jnp.float32, jnp.bfloat16
 NT = 25
-SEMS = 60
+SEMS = 58
 
 
 MESH = pl.DeviceIdType.MESH
@@ -197,68 +197,60 @@
             paired[i] = paired[i] + grads[i, :, k.c, t_base : t_base + n_tiles]
 
         for half in (0, 1):
-            spread(half, 0) if direct else outset(half)
-
-    def spread(half, step):
-        box = (first_in if step == 0 else second_in)[half]
-        sem = sems[half, step] = k.take()
+            outset(half)
+
+    def spread(half):
+        box = second_in[half]
+        sem = sems[half, 1] = k.take()
         for d in (2, 1, 3):
-            k.copy(view(half, step, d), box.at[d - 1], to_axis(half, step, d), sem).start()
+            k.copy(view(half, 1, d), box.at[d - 1], to_axis(half, 1, d), sem).start()
         k.later(box, sem)
 
-    def collect_spread(half, step):
-        box = (first_in if step == 0 else second_in)[half]
-        k.arrived(box, sems[half, step])
-        own = view(half, step, 0)
+    def collect_spread(half):
+        box = second_in[half]
+        k.arrived(box, sems[half, 1])
+        own = view(half, 1, 0)
         near = box[0].astype(f32) + box[2].astype(f32)
         own[...] = ((own[...].astype(f32) + box[1].astype(f32)) + near).astype(jnp.bfloat16)
 
+    ways = ((0, 1), (1, -1))
+
     def outset(half):
-        one, two = first_in[half][:2], first_in[half][2:]
-        base = sems[half, 0] = k.take(4)
-        for direction, delta in ((0, 1), (1, -1)):
-            k.copy(
-                view(half, 0, 2, direction), one[direction], to_axis(half, 0, delta), base + direction
-            ).start()
-            k.later(one[direction], base + direction)
-        for direction, delta in ((0, 1), (1, -1)):
-            part = 1 - direction
-            k.copy(
-                view(half, 0, delta, part),
-                two[direction].at[2 * part : 2 * part + 2],
-                to_axis(half, 0, delta),
-                base + 2 + direction,
-            ).start()
+        one, two = first_in[half]
+        base = sems[half, 0] = k.take(2)
+        for way, delta in ways:
+            target = to_axis(half, 0, delta)
+            k.copy(view(half, 0, 2, way), one.at[way], target, base).start()
+        for way, delta in ways:
+            part = 1 - way
+            box = two.at[way, 2 * part : 2 * part + 2]
+            k.copy(view(half, 0, delta, part), box, to_axis(half, 0, delta), base + 1).start()
+        k.later(one, base)
 
     def relay():
         for half in (0, 1):
-            one, two = first_in[half][:2], first_in[half][2:]
+            one, two = first_in[half]
             base = sems[half, 0]
-            for direction, delta in ((0, 1), (1, -1)):
-                k.arrived(one[direction], base + direction)
-                target = view(half, 0, delta, direction)
-                target[...] = target[...] + one[direction][...]
-                k.copy(
-                    target,
-                    two[direction].at[2 * direction : 2 * direction + 2],
-                    to_axis(half, 0, delta),
-                    base + 2 + direction,
-                ).start()
-                k.later(two[direction], base + 2 + direction)
+            k.arrived(one, base)
+            for way, delta in ways:
+                target = view(half, 0, delta, way)
+                target[...] = target[...] + one[way]
+                box = two.at[way, 2 * way : 2 * way + 2]
+                k.copy(target, box, to_axis(half, 0, delta), base + 1).start()
+            k.later(two, base + 1)
 
     def collect(half):
-        two = first_in[half][2:]
-        for direction in (0, 1):
-            k.arrived(two[direction], sems[half, 0] + 2 + direction)
+        two = first_in[half][1]
+        k.arrived(two, sems[half, 0] + 1)
         own = view(half, 0, 0)
-        own[...] = (
-            own[...].astype(f32) + (two[0][...].astype(f32) + two[1][...].astype(f32))
-        ).astype(jnp.bfloat16)
+        own[...] = (own[...].astype(f32) + (two[0].astype(f32) + two[1].astype(f32))).astype(
+            jnp.bfloat16
+        )
 
     def turn():
         for half in (0, 1):
-            collect_spread(half, 0) if direct else collect(half)
-            spread(half, 1)
+            collect(half)
+            spread(half)
 
     spot = 2 * k.zh + k.zl
     holds = k.zl == k.c
@@ -266,7 +258,7 @@
 
     def z_out():
         for half in (0, 1):
-            collect_spread(half, 1)
+            collect_spread(half)
         sem = sems["z"] = k.take()
         for q in range(4):
             for e in range(2):
@@ -309,7 +301,7 @@
 
     def whole_out():
         for half in (0, 1):
-            collect_spread(half, 1)
+            collect_spread(half)
         sem = sems["z"] = k.take()
         for q in range(4):
             op = k.copy(paired.at[k.x, k.y], z_in.at[spot], k.at(zl=k.c, zh=q), sem)
@@ -343,7 +335,7 @@
 
     pairs = [functools.partial(pair_out, i) for i in range(len(cuts) - 1)]
     if direct:
-        return pairs + [pair_in, turn, whole_out, whole_sum, whole_in]
+        return pairs + [pair_in, relay, turn, whole_out, whole_sum, whole_in]
     return pairs + [pair_in, relay, turn, z_out, z_sum, gather]
 
 
@@ -368,20 +360,16 @@
         return pltpu.VMEM((*lead, 16, 128), jnp.bfloat16)
 
     shapes = [tiles(4, 4, n_tiles)]
+    for _, n in halves_of(n_tiles):
+        shapes += [tiles(2, 2, n), tiles(2, 4, n)]
+    shapes += [tiles(3, n) for _, n in halves_of(n_tiles)]
     if direct:
-        for lead in ((3, 4), (3,)):
-            shapes += [tiles(*lead, n) for _, n in halves_of(n_tiles)]
         return shapes + [tiles(8, n_tiles), tiles(1, n_tiles)]
-    for _, n in halves_of(n_tiles):
-        shapes += [tiles(2, n)] * 2 + [tiles(4, n)] * 2
-    shapes += [tiles(3, n) for _, n in halves_of(n_tiles)]
     return shapes + [tiles(8, pieces_of(n_tiles)[1])] * 2
 
 
-def sum_refs(refs, direct):
-    if direct:
-        return refs[0], refs[1:3], refs[3:5], refs[5], refs[6]
-    return refs[0], (refs[1:5], refs[5:9]), refs[9:11], refs[11], refs[12]
+def sum_refs(refs):
+    return refs[0], (refs[1:3], refs[3:5]), refs[5:7], refs[7], refs[8]
 
 
 NN = (((1,), (0,)), ((), ()))
@@ -576,7 +564,7 @@
     sums = []
     for _, cuts, direct in GROUPS:
         count = len(sum_scratch(cuts, direct))
-        sums.append(sum_refs(refs[:count], direct))
+        sums.append(sum_refs(refs[:count]))
         refs = refs[count:]
     small_bufs = refs[0]
     local, send, recv = refs[1:4]
@@ -704,6 +692,10 @@
             m.back_pos[h] = backward_input(m, 1, h, x, upstream).reshape(16, 16, D)
         send(back_copy, h)
         m.back[:, p, h] = m.back_pos[h, pl.ds(2 * p, 2)]
+
+    def attention_0(g):
+        with jax.named_scope("attn0"):
+            backward_attention(m, 0, g)
 
     def input_0(g):
         with jax.named_scope("input0"):
@@ -736,26 +728,25 @@
         send(out_copy, h)
     with jax.named_scope("wgo0"):
         weight_out_grad(m, 0, m.back[...].reshape(2 * BLOCK, D))
-    run("a0")
+    run("a0 b1")
     with jax.named_scope("gate0"):
         for g in (0, 1):
             backward_gate(m, 0, g, m.back[g].reshape(BLOCK, D))
-    run("b1")
     with jax.named_scope("wgi0"):
         weight_in_grad(m, 0, GATE)
     run("a0 a1")
-    with jax.named_scope("attn0"):
-        for g in (0, 1):
-            backward_attention(m, 0, g)
-    run("b1 a0")
+    attention_0(0)
+    run("a0")
+    attention_0(1)
+    run("b1")
     with jax.named_scope("wg0b"):
         weight_in_grad(m, 0, OTHERS)
-    run("b0")
+    run("b0 a1")
     input_0(0)
-    run("a1")
+    run("a0")
     input_0(1)
     store_back = load(m.back_frames, back_hbm, 0)
-    run("s b0 a0 s b1 b0 a0 s a1 b1 b0 a0 s")
+    run("b0 s b1 s a0 b0 b0 a0 a1 b1 s b0 s")
     with jax.named_scope("w_out"):
         receive(out_sems, 0)
         receive(out_sems, 1)

time: 86.5 us -> 83.7 us (0.968)
  Pallas kernels: 85.7 us -> 82.9 us
    pallas_call x1, Pallas kernels: 83.3 us -> 80.5 us  [on_device(): pl.pallas_call(functools.partial(step_kernel, tokens_all ** (-0.5)), out_...]
where the time goes in v5:
time: 83.7 us; the launch traced here: 83.6 us
  Pallas kernels  82.9 us (99%)
    pallas_call x1, Pallas kernels, on_device(): pl.pallas_call(functools.partial(step_kernel, tokens_all ** (-0.5)), out_...  80.5 us
    pallas_call x1, Pallas kernels, on_device(): pl.pallas_call(write_kernel, out_shape=(jax.ShapeDtypeStruct(frames.shape...  2.45 us

profile of v5, /device:TPU:1, one launch (start us, length us, event | category | flops | bytes accessed | tf_op | source)
XLA Modules:
  0.0 83.6 jit_solution(10328302731512433119)
XLA Ops:
  0.6 80.5 %shard_map.109 = (bf16[2,8,2,16,512]{4,3,2,1,0:T(8,128)(2,1)}, bf16[2,256,512]{2,1,0:T(8,128)(2,1)}, f32[2,16,2176]{2,1,0:T(8,128)}, f32[2,32,512]{2,1,0:T(8,128)}, f32[2,8,128]{2,1,0:T(8,128)}) custom-call(bf16[2,256,512]{2,1,0:T(8,128)(2,1)} %bitcast.2, bf16[2,8,2,16,512]{4,3,2,1,0:T(8,128)(2,1)} %bitcast.3, bf16[2,512,2176]{2,1,0:T(8,128)(2,1)} %refs_2_.1, ...), custom_call_target="tpu_custom_call" | custom-call | tf_op jit(solution)/shard_map/pallas_call | solution.py:796
  81.1 2.5 %shard_map.110 = (bf16[1,512,512]{2,1,0:T(8,128)(2,1)}, bf16[1,512,512]{2,1,0:T(8,128)(2,1)}, f32[2,16,2176]{2,1,0:T(8,128)}, f32[2,32,512]{2,1,0:T(8,128)}, f32[2,512]{1,0:T(2,128)}, /*index=5*/f32[2,2,128]{2,1,0:T(2,128)}) custom-call(bf16[2,8,2,16,512]{4,3,2,1,0:T(8,128)(2,1)} %get-tuple-element.11.result, bf16[2,256,512]{2,1,0:T(8,128)(2,1)} %get-tuple-element.12.back, ...), custom_call_target="tpu_custom_call" | custom-call | tf_op jit(solution)/shard_map/pallas_call | solution.py:819

commit v6 on v5

--- a/solution.py
+++ b/solution.py
@@ -192,11 +192,13 @@
         for i in range(len(cuts) - 1):
             pair_copy(i).wait_recv()
 
-        @pl.loop(0, 4)
-        def _(i):
-            paired[i] = paired[i] + grads[i, :, k.c, t_base : t_base + n_tiles]
-
-        for half in (0, 1):
+        for half, (t0, n) in enumerate(halves):
+
+            @pl.loop(0, 4)
+            def _(i):
+                own = grads[i, :, k.c, t_base + t0 : t_base + t0 + n]
+                paired[i, :, t0 : t0 + n] = paired[i, :, t0 : t0 + n] + own
+
             outset(half)
 
     def spread(half):
@@ -608,9 +610,8 @@
         box = m.out.at[:, p, h]
         return k.copy(m.out_pos.at[h, pl.ds(2 * to[0], 2)], box, to[1], out_sems + h)
 
-    def back_copy(h, d, to):
-        box = m.back.at[:, p, h]
-        return k.copy(m.back_pos.at[h, pl.ds(2 * to[0], 2)], box, to[1], back_sems + h)
+    def back_copy(b, h, d, to):
+        return k.copy(m.back_pos.at[h, 2 * to[0] + b], m.back.at[b, p, h], to[1], back_sems + b)
 
     def send(copy, h):
         for d in range(1, 8):
@@ -690,8 +691,16 @@
             x = m.first_pos[h].reshape(BLOCK, D)
             upstream = m.cot_pos[h].reshape(BLOCK, D)
             m.back_pos[h] = backward_input(m, 1, h, x, upstream).reshape(16, 16, D)
-        send(back_copy, h)
+        for b in (0, 1):
+            send(functools.partial(back_copy, b), h)
         m.back[:, p, h] = m.back_pos[h, pl.ds(2 * p, 2)]
+
+    def gate_0(g, wait=True):
+        if wait:
+            with jax.named_scope("w_back"):
+                receive(back_sems, g)
+        with jax.named_scope("gate0"):
+            backward_gate(m, 0, g, m.back[g].reshape(BLOCK, D))
 
     def attention_0(g):
         with jax.named_scope("attn0"):
@@ -721,17 +730,15 @@
     with jax.named_scope("wg1b"):
         weight_in_grad(m, 1, OTHERS)
     run("b1 b1 a1")
-    with jax.named_scope("w_back"):
-        receive(back_sems, 0)
+    gate_0(0)
+    with jax.named_scope("w_back1"):
         receive(back_sems, 1)
     for h in (0, 1):
         send(out_copy, h)
     with jax.named_scope("wgo0"):
         weight_out_grad(m, 0, m.back[...].reshape(2 * BLOCK, D))
     run("a0 b1")
-    with jax.named_scope("gate0"):
-        for g in (0, 1):
-            backward_gate(m, 0, g, m.back[g].reshape(BLOCK, D))
+    gate_0(1, False)
     with jax.named_scope("wgi0"):
         weight_in_grad(m, 0, GATE)
     run("a0 a1")

time: 83.7 us -> 82 us (0.980)
  Pallas kernels: 82.9 us -> 81.3 us
    pallas_call x1, Pallas kernels: 80.5 us -> 78.8 us  [on_device(): pl.pallas_call(functools.partial(step_kernel, tokens_all ** (-0.5)), out_...]
where the time goes in v6:
time: 82 us; the launch traced here: 81.9 us
  Pallas kernels  81.3 us (99%)
    pallas_call x1, Pallas kernels, on_device(): pl.pallas_call(functools.partial(step_kernel, tokens_all ** (-0.5)), out_...  78.8 us
    pallas_call x1, Pallas kernels, on_device(): pl.pallas_call(write_kernel, out_shape=(jax.ShapeDtypeStruct(frames.shape...  2.45 us

profile of v6, /device:TPU:1, one launch (start us, length us, event | category | flops | bytes accessed | tf_op | source)
XLA Modules:
  0.0 81.9 jit_solution(5845456162699398432)
XLA Ops:
  0.6 78.8 %shard_map.109 = (bf16[2,8,2,16,512]{4,3,2,1,0:T(8,128)(2,1)}, bf16[2,256,512]{2,1,0:T(8,128)(2,1)}, f32[2,16,2176]{2,1,0:T(8,128)}, f32[2,32,512]{2,1,0:T(8,128)}, f32[2,8,128]{2,1,0:T(8,128)}) custom-call(bf16[2,256,512]{2,1,0:T(8,128)(2,1)} %bitcast.2, bf16[2,8,2,16,512]{4,3,2,1,0:T(8,128)(2,1)} %bitcast.3, bf16[2,512,2176]{2,1,0:T(8,128)(2,1)} %refs_2_.1, ...), custom_call_target="tpu_custom_call" | custom-call | tf_op jit(solution)/shard_map/pallas_call | solution.py:803
  79.5 2.5 %shard_map.110 = (bf16[1,512,512]{2,1,0:T(8,128)(2,1)}, bf16[1,512,512]{2,1,0:T(8,128)(2,1)}, f32[2,16,2176]{2,1,0:T(8,128)}, f32[2,32,512]{2,1,0:T(8,128)}, f32[2,512]{1,0:T(2,128)}, /*index=5*/f32[2,2,128]{2,1,0:T(2,128)}) custom-call(bf16[2,8,2,16,512]{4,3,2,1,0:T(8,128)(2,1)} %get-tuple-element.11.result, bf16[2,256,512]{2,1,0:T(8,128)(2,1)} %get-tuple-element.12.back, ...), custom_call_target="tpu_custom_call" | custom-call | tf_op jit(solution)/shard_map/pallas_call | solution.py:826

commit v7 on v6

--- a/solution.py
+++ b/solution.py
@@ -779,15 +779,30 @@
     assert k.used <= SEMS
 
 
-def write_kernel(result, back, grad_in, grad_out, small, o_result, o_back, o_in, o_out, o_gains, o_scales):
-    o_result[...] = result[...].reshape(o_result.shape)
-    o_back[...] = back[...].reshape(o_back.shape)
-    o_in[...] = grad_in[...]
-    o_out[...] = grad_out[...]
+def write_kernel(*refs):
+    arrived, outputs, held = refs[:5], refs[5:11], refs[11:18]
+    come, gone = refs[18:]
+    incoming = [pltpu.make_async_copy(arrived[i], held[i], come.at[i]) for i in range(5)]
+    for i in (4, 3, 2, 1, 0):
+        incoming[i].start()
+    outgoing = [pltpu.make_async_copy(held[i], outputs[i], gone.at[i]) for i in range(4)]
+    small, gains, scales = held[4:]
+    outgoing += [
+        pltpu.make_async_copy(gains, outputs[4], gone.at[4]),
+        pltpu.make_async_copy(scales, outputs[5], gone.at[5]),
+    ]
+    incoming[4].wait()
     for unit in (0, 1):
         for i in range(4):
-            o_gains[unit : unit + 1, 128 * i : 128 * i + 128] = small[unit, i : i + 1, :]
-        o_scales[unit] = small[unit, 4:6, :]
+            gains[unit : unit + 1, 128 * i : 128 * i + 128] = small[unit, i : i + 1, :]
+        scales[unit] = small[unit, 4:6, :]
+    outgoing[4].start()
+    outgoing[5].start()
+    for i in (3, 2, 1, 0):
+        incoming[i].wait()
+        outgoing[i].start()
+    for op in outgoing:
+        op.wait()
 
 
 def on_device(frames, cotangent, weight_in, qk_scales, weight_out, gains):
@@ -823,19 +838,23 @@
         qk_scales,
         gains,
     )
-    return pl.pallas_call(
+    shapes = [(part.shape, part.dtype) for part in parts]
+    small_shapes = [((2, D), F32), ((2, 2, S), F32)]
+    result, back, grad_in, grad_out, gains_sum, scales_sum = pl.pallas_call(
         write_kernel,
-        out_shape=(
-            jax.ShapeDtypeStruct(frames.shape, BF16),
-            jax.ShapeDtypeStruct(frames.shape, BF16),
-            jax.ShapeDtypeStruct((2, 16, WIDE), F32),
-            jax.ShapeDtypeStruct((2, 32, D), F32),
-            jax.ShapeDtypeStruct((2, D), F32),
-            jax.ShapeDtypeStruct((2, 2, S), F32),
-        ),
-        in_specs=[vmem] * 5,
-        out_specs=(vmem,) * 6,
+        out_shape=tuple(jax.ShapeDtypeStruct(*one) for one in shapes[:4] + small_shapes),
+        in_specs=[hbm] * 5,
+        out_specs=(hbm,) * 6,
+        scratch_shapes=[pltpu.VMEM(*one) for one in shapes + small_shapes] + [dma((5,)), dma((6,))],
     )(*parts)
+    return (
+        result.reshape(frames.shape),
+        back.reshape(frames.shape),
+        grad_in,
+        grad_out,
+        gains_sum,
+        scales_sum,
+    )
 
 
 def solution(mesh):

time: 82 us -> 82.1 us (level)
  no operation moved by 1% of the time
where the time goes in v7:
time: 82.1 us; the launch traced here: 81.9 us
  Pallas kernels  81.1 us (99%)
    pallas_call x1, Pallas kernels, on_device(): pl.pallas_call(functools.partial(step_kernel, tokens_all ** (-0.5)), out_...  78.8 us
    pallas_call x1, Pallas kernels, on_device(): pl.pallas_call(write_kernel, out_shape=tuple((jax.ShapeDtypeStruct(*one)...  2.28 us

profile of v7, /device:TPU:1, one launch (start us, length us, event | category | flops | bytes accessed | tf_op | source)
XLA Modules:
  0.0 81.9 jit_solution(14798851948693457290)
XLA Ops:
  0.6 78.8 %shard_map.109 = (bf16[2,8,2,16,512]{4,3,2,1,0:T(8,128)(2,1)}, bf16[2,256,512]{2,1,0:T(8,128)(2,1)}, f32[2,16,2176]{2,1,0:T(8,128)}, f32[2,32,512]{2,1,0:T(8,128)}, f32[2,8,128]{2,1,0:T(8,128)}) custom-call(bf16[2,256,512]{2,1,0:T(8,128)(2,1)} %bitcast.4, bf16[2,8,2,16,512]{4,3,2,1,0:T(8,128)(2,1)} %bitcast.5, bf16[2,512,2176]{2,1,0:T(8,128)(2,1)} %refs_2_.1, ...), custom_call_target="tpu_custom_call" | custom-call | tf_op jit(solution)/shard_map/pallas_call | solution.py:818
  79.5 2.3 %shard_map.110 = (bf16[2,8,2,16,512]{4,3,2,1,0:T(8,128)(2,1)}, bf16[2,256,512]{2,1,0:T(8,128)(2,1)}, f32[2,16,2176]{2,1,0:T(8,128)}, f32[2,32,512]{2,1,0:T(8,128...) custom-call(bf16[2,8,2,16,512]{4,3,2,1,0:T(8,128)(2,1)} %get-tuple-element.17.refs_0_, ...), custom_call_target="tpu_custom_call" | custom-call | tf_op jit(solution)/shard_map/pallas_call | solution.py:843
